TPU v7x, 32 devices: a whole 2x2x4 slice. The times are simulated.
32 devices in a mesh: dp: 16 (over z, x, core), fsdp: 2 (over y).
Axes of the slice: x: 2, y: 2, z: 4, core: 2. Of those that a mesh axis runs over, the one named last changes fastest.
Arguments:
- hidden: bfloat16 [64, 512, 768], P(('dp', 'fsdp')), may hold values from -7 to 7
- lengths: int32 [64], P(('dp', 'fsdp')), may hold values from 1 to 512, 20480 in all
- in_weight: bfloat16 [768, 1536], P(('dp', 'fsdp')), may hold values from -0.21875 to 0.21875
- depth_kernel: bfloat16 [9, 768], P(None, ('dp', 'fsdp')), may hold values from -2 to 2
- point_weight: bfloat16 [768, 384], P(('dp', 'fsdp')), may hold values from -0.21875 to 0.21875
- kernel_weight: bfloat16 [9, 2304], P(None, ('dp', 'fsdp')), may hold values from -0.3125 to 0.3125
- out_weight: bfloat16 [768, 768], P(('dp', 'fsdp')), may hold values from -0.875 to 0.875
- up_weight: bfloat16 [2, 384, 1536], P(None, None, ('dp', 'fsdp')), may hold values from -0.3125 to 0.3125
- down_weight: bfloat16 [2, 1536, 384], P(None, ('dp', 'fsdp')), may hold values from -0.15625 to 0.15625
- norm_gains: bfloat16 [2, 768], P(None, ('dp', 'fsdp')), may hold values from 0.25 to 1.75
- norm_biases: bfloat16 [2, 768], P(None, ('dp', 'fsdp')), may hold values from -3 to 3
- out_grad: bfloat16 [64, 512, 768], P(('dp', 'fsdp')), may hold values from -6 to 6
Outputs:
- output: bfloat16 [64, 512, 768], P(('dp', 'fsdp'))
- input_grad: bfloat16 [64, 512, 768], P(('dp', 'fsdp'))
- grad_in_weight: float32 [768, 1536], P(('dp', 'fsdp'))
- grad_depth_kernel: float32 [9, 768], P(None, ('dp', 'fsdp'))
- grad_point_weight: float32 [768, 384], P(('dp', 'fsdp'))
- grad_kernel_weight: float32 [9, 2304], P(None, ('dp', 'fsdp'))
- grad_out_weight: float32 [768, 768], P(('dp', 'fsdp'))
- grad_up_weight: float32 [2, 384, 1536], P(None, None, ('dp', 'fsdp'))
- grad_down_weight: float32 [2, 1536, 384], P(None, ('dp', 'fsdp'))
- grad_norm_gains: float32 [2, 768], P(None, ('dp', 'fsdp'))
- grad_norm_biases: float32 [2, 768], P(None, ('dp', 'fsdp'))
- rms: float32 [4], replicated
All inputs are finite; a program needn't handle non-finite values. No bound on the sum of `lengths` on one device may be relied on, other than what follows from the above.
Results may differ from a plain program's by a relative error of at most 0.015.
Values may be sent and summed in bfloat16 or wider, within the bound.
A program may use at most 192 MiB of HBM per device.

v0:
```python
import functools
import math

import jax
import jax.numpy as jnp
from jax import lax
from jax.experimental import pallas as pl
from jax.experimental.pallas import tpu as pltpu
from jax.sharding import PartitionSpec as P

D = 768
HEADS = 6
HD = 64
G = 2
K = 9
SEQ = 512


EPSILON = 1e-06
MESH = pl.DeviceIdType.MESH
BLOCKS = 16
HALF = BLOCKS // 2


def place():
    dp, y = lax.axis_index("dp"), lax.axis_index("fsdp")
    return dp, dp // 4, (dp // 2) % 2, dp % 2, y


def partners(dp, x, core, y):
    return (dp + 1 - 2 * core, y), (dp + 2 - 4 * x, y), (dp, 1 - y)


def meet(peers, others):
    barrier = pltpu.get_barrier_semaphore()
    for peer in peers:
        pl.semaphore_signal(barrier, inc=1, device_id=peer, device_id_type=MESH)
    count = len(peers)
    for there, peer in others:

        @pl.when(there)
        def _():
            pl.semaphore_signal(barrier, inc=1, device_id=peer, device_id_type=MESH)

        count = count + there.astype(jnp.int32)
    pl.semaphore_wait(barrier, count)


def send(src, dst, send_sem, recv_sem, device):
    return pltpu.make_async_remote_copy(
        src_ref=src,
        dst_ref=dst,
        send_sem=send_sem,
        recv_sem=recv_sem,
        device_id=device,
        device_id_type=MESH,
    )


def gather_kernel(
    depth, p_ref, g_ref, own_sem, zs, zr, xs, xr, ys, yr, ds, dr, cs, cr
):
    dp, z, x, core, y = place()
    c_dev, x_dev, y_dev = partners(dp, x, core, y)
    up_dev, down_dev = (dp + 4, y), (dp - 4, y)
    own = pltpu.make_async_copy(p_ref, g_ref.at[:, z, x, core, y], own_sem)
    own.start()
    meet((c_dev, x_dev, y_dev), ((z + 1 < depth, up_dev), (z > 0, down_dev)))
    own.wait()
    steps = 2 * depth - 1

    def target(q):
        return z + ((q + 1) // 2) * (1 - 2 * (q % 2))

    def z_copy(j, way, device):
        slab = g_ref.at[:, j, x, core, y]
        return send(slab, slab, zs.at[way, j], zr.at[j], device)

    def x_copy(j):
        slab = g_ref.at[:, j, x, core, y]
        return send(slab, slab, xs.at[j], xr.at[j], x_dev)

    def y_copy(j):
        slab = g_ref.at[:, j, x, core, y]
        return send(slab, slab, ys.at[j], yr.at[j], y_dev)

    def d_copy(j, half):
        if half == 0:
            slab = g_ref.at[pl.ds(0, HALF), j, 1 - x, core, y]
            return send(slab, slab, ds.at[0, j], dr.at[0, j], y_dev)
        slab = g_ref.at[pl.ds(HALF, HALF), j, x, core, 1 - y]
        return send(slab, slab, ds.at[1, j], dr.at[1, j], x_dev)

    def c_copy(j, a, b):
        slab = g_ref.at[:, j, (x + a) % 2, core, (y + b) % 2]
        return send(slab, slab, cs.at[2 * a + b, j], cr.at[2 * a + b, j], c_dev)

    def c_arrival(j, a, b):
        slab = g_ref.at[:, j, (x + a) % 2, 1 - core, (y + b) % 2]
        return send(slab, slab, cs.at[2 * a + b, j], cr.at[2 * a + b, j], c_dev)

    def x_arrival(j):
        slab = g_ref.at[:, j, 1 - x, core, y]
        return send(slab, slab, xs.at[j], xr.at[j], x_dev)

    def y_arrival(j):
        slab = g_ref.at[:, j, x, core, 1 - y]
        return send(slab, slab, ys.at[j], yr.at[j], y_dev)

    def d_arrival(j, half):
        slab = g_ref.at[pl.ds(half * HALF, HALF), j, 1 - x, core, 1 - y]
        return send(slab, slab, ds.at[half, j], dr.at[half, j], y_dev if half == 0 else x_dev)

    def first(j):
        @pl.when(j != z)
        def _():
            z_copy(j, 0, up_dev).wait_recv()

        @pl.when((j <= z) & (z + 1 < depth))
        def _():
            z_copy(j, 0, up_dev).start()

        @pl.when((j >= z) & (z > 0))
        def _():
            z_copy(j, 1, down_dev).start()

        x_copy(j).start()
        y_copy(j).start()
        c_copy(j, 0, 0).start()

    def second(j):
        x_arrival(j).wait_recv()
        d_copy(j, 0).start()
        c_copy(j, 1, 0).start()
        y_arrival(j).wait_recv()
        d_copy(j, 1).start()
        c_copy(j, 0, 1).start()

    def third(j):
        d_arrival(j, 0).wait_recv()
        d_arrival(j, 1).wait_recv()
        c_copy(j, 1, 1).start()

    def stage(q, work):
        j = target(q)

        @pl.when((q >= 0) & (q < steps) & (j >= 0) & (j < depth))
        def _():
            work(j)

    def step(q, carry):
        stage(q, first)
        stage(q - 1, second)
        stage(q - 2, third)
        return carry

    lax.fori_loop(0, steps + 2, step, 0)

    def finish(j, carry):
        for a in range(2):
            for b in range(2):
                c_arrival(j, a, b).wait_recv()
                c_copy(j, a, b).wait_send()
        x_copy(j).wait_send()
        y_copy(j).wait_send()
        d_copy(j, 0).wait_send()
        d_copy(j, 1).wait_send()

        @pl.when((j <= z) & (z + 1 < depth))
        def _():
            z_copy(j, 0, up_dev).wait_send()

        @pl.when((j >= z) & (z > 0))
        def _():
            z_copy(j, 1, down_dev).wait_send()

        return carry

    lax.fori_loop(0, depth, finish, 0)


def gather_all(packed, mesh):
    dp, fsdp = mesh.shape["dp"], mesh.shape["fsdp"]
    _, rows, width = packed.shape
    if fsdp != 2 or dp % 4:
        full = lax.all_gather(packed, ("dp", "fsdp"), axis=1, tiled=False)
        return full.reshape(BLOCKS, dp * fsdp * rows, width)
    depth = dp // 4
    dma = pltpu.SemaphoreType.DMA
    full = pl.pallas_call(
        functools.partial(gather_kernel, depth),
        out_shape=jax.ShapeDtypeStruct((BLOCKS, depth, 2, 2, 2, rows, width), packed.dtype),
        in_specs=[pl.BlockSpec(memory_space=pltpu.VMEM)],
        out_specs=pl.BlockSpec(memory_space=pl.ANY),
        scratch_shapes=[
            dma(()),
            dma((2, depth)),
            dma((depth,)),
            dma((depth,)),
            dma((depth,)),
            dma((depth,)),
            dma((depth,)),
            dma((2, depth)),
            dma((2, depth)),
            dma((4, depth)),
            dma((4, depth)),
        ],
        compiler_params=pltpu.CompilerParams(collective_id=0, has_side_effects=True),
        name="gather_all",
    )(packed)
    return full.reshape(BLOCKS, dp * fsdp * rows, width)


def scatter_kernel(
    depth,
    l_ref,
    t_ref,
    o_ref,
    u_ref,
    acc,
    rc,
    ry1,
    rx1,
    rx2,
    ry2,
    rup,
    rdn,
    tiny,
    got,
    load_sem,
    cs,
    cr,
    ss,
    sr,
    zs,
    zr,
    ts,
    tr,
):
    dp, z, x, core, y = place()
    c_dev, x_dev, y_dev = partners(dp, x, core, y)
    up_dev, down_dev = (dp + 4, y), (dp - 4, y)
    steps = 2 * depth - 1
    bf16, f32 = jnp.bfloat16, jnp.float32

    def target(q):
        return z + (depth - 1 - q // 2) * (1 - 2 * (q % 2))

    def valid(q):
        j = target(q)
        return (q >= 0) & (q < steps) & (j >= 0) & (j < depth)

    def load(j):
        return pltpu.make_async_copy(l_ref.at[:, j, :, core, :], acc.at[j], load_sem.at[j])

    def c_copy(j):
        return send(l_ref.at[:, j, :, 1 - core, :], rc.at[j], cs.at[j], cr.at[j], c_dev)

    def y1_copy(j):
        return send(acc.at[j, pl.ds(0, HALF), :, 1 - y], ry1.at[j], ss.at[0, j], sr.at[0, j], y_dev)

    def x1_copy(j):
        return send(acc.at[j, pl.ds(HALF, HALF), 1 - x], rx1.at[j], ss.at[1, j], sr.at[1, j], x_dev)

    def x2_copy(j):
        return send(acc.at[j, pl.ds(0, HALF), 1 - x, y], rx2.at[j], ss.at[2, j], sr.at[2, j], x_dev)

    def y2_copy(j):
        return send(acc.at[j, pl.ds(HALF, HALF), x, 1 - y], ry2.at[j], ss.at[3, j], sr.at[3, j], y_dev)

    def up_copy(j):
        return send(acc.at[j, :, x, y], rup.at[j], zs.at[j], zr.at[0, j], up_dev)

    def down_copy(j):
        return send(acc.at[j, :, x, y], rdn.at[j], zs.at[j], zr.at[1, j], down_dev)

    def issue(q, carry):
        @pl.when(valid(q))
        def _():
            load(target(q)).start()

        return carry

    lax.fori_loop(0, steps, issue, 0)
    lines = tuple((z >= d, (dp - 4 * d, y)) for d in range(1, depth)) + tuple(
        (z + d < depth, (dp + 4 * d, y)) for d in range(1, depth)
    )
    meet((c_dev, x_dev, y_dev), lines)

    def issue_core(q, carry):
        @pl.when(valid(q))
        def _():
            c_copy(target(q)).start()

        return carry

    lax.fori_loop(0, steps, issue_core, 0)

    tiny[0] = t_ref[...]

    def t_copy(k):
        return send(tiny.at[k], got.at[k], ts.at[k], tr.at[k], (c_dev, x_dev, y_dev)[k])

    def t_line(d, way):
        return send(
            tiny.at[3],
            got.at[3 + z],
            ts.at[2 + d if way > 0 else 1 + depth + d],
            tr.at[3 + z],
            (dp + 4 * d * way, y),
        )

    def t_arrival(level):
        return send(tiny.at[3], got.at[3 + level], ts.at[0], tr.at[3 + level], c_dev)

    t_copy(0).start()

    def add(into, other):
        return (into.astype(f32) + other.astype(f32)).astype(bf16)

    def first(j):
        load(j).wait()
        c_copy(j).wait_recv()

        def block(b, carry):
            acc[j, b] = add(acc[j, b], rc[j, b])
            return carry

        lax.fori_loop(0, BLOCKS, block, 0)
        y1_copy(j).start()
        x1_copy(j).start()

    def second(j):
        y1_copy(j).wait_recv()

        def low(b, carry):
            for a in range(2):
                acc[j, b, a, y] = add(acc[j, b, a, y], ry1[j, b, a])
            return carry

        lax.fori_loop(0, HALF, low, 0)
        x2_copy(j).start()
        x1_copy(j).wait_recv()

        def high(b, carry):
            for a in range(2):
                acc[j, HALF + b, x, a] = add(acc[j, HALF + b, x, a], rx1[j, b, a])
            return carry

        lax.fori_loop(0, HALF, high, 0)
        y2_copy(j).start()

    def third(j):
        x2_copy(j).wait_recv()
        y2_copy(j).wait_recv()

        @pl.when((j >= z) & (z > 0))
        def _():
            up_copy(j).wait_recv()

        @pl.when((j <= z) & (z + 1 < depth))
        def _():
            down_copy(j).wait_recv()

        def block(b, carry):
            for part, other in ((0, rx2), (HALF, ry2)):
                total = acc[j, part + b, x, y].astype(f32) + other[j, b].astype(f32)

                @pl.when(j == z)
                def _():
                    o_ref[part + b] = total

                @pl.when(j != z)
                def _():
                    acc[j, part + b, x, y] = total.astype(bf16)

            return carry

        lax.fori_loop(0, HALF, block, 0)

        def more(ref, low_precision):
            def block(b, carry):
                if low_precision:
                    acc[j, b, x, y] = add(acc[j, b, x, y], ref[j, b])
                else:
                    o_ref[b] = o_ref[b] + ref[j, b].astype(f32)
                return carry

            lax.fori_loop(0, BLOCKS, block, 0)

        @pl.when((j > z) & (z > 0))
        def _():
            more(rup, True)

        @pl.when((j < z) & (z + 1 < depth))
        def _():
            more(rdn, True)

        @pl.when((j == z) & (z > 0))
        def _():
            more(rup, False)

        @pl.when((j == z) & (z + 1 < depth))
        def _():
            more(rdn, False)

        @pl.when(j > z)
        def _():
            up_copy(j).start()

        @pl.when(j < z)
        def _():
            down_copy(j).start()

    def stage(q, work):
        @pl.when(valid(q))
        def _():
            work(target(q))

    def step(q, carry):
        stage(q, first)
        stage(q - 1, second)
        stage(q - 2, third)
        return carry

    lax.fori_loop(0, steps + 2, step, 0)

    for k in range(3):
        t_copy(k).wait_recv()
        tiny[k + 1] = tiny[k] + got[k]
        if k < 2:
            t_copy(k + 1).start()
    for d in range(1, depth):

        @pl.when(z + d < depth)
        def _():
            t_line(d, 1).start()

        @pl.when(z >= d)
        def _():
            t_line(d, -1).start()

    for level in range(depth):

        @pl.when(z == level)
        def _():
            got[3 + level] = tiny[3]

        @pl.when(z != level)
        def _():
            t_arrival(level).wait_recv()

    total = got[3]
    for level in range(1, depth):
        total = total + got[3 + level]
    u_ref[...] = total

    for d in range(1, depth):

        @pl.when(z + d < depth)
        def _():
            t_line(d, 1).wait_send()

        @pl.when(z >= d)
        def _():
            t_line(d, -1).wait_send()

    for k in range(3):
        t_copy(k).wait_send()

    def finish(j, carry):
        c_copy(j).wait_send()
        y1_copy(j).wait_send()
        x1_copy(j).wait_send()
        x2_copy(j).wait_send()
        y2_copy(j).wait_send()

        @pl.when(j > z)
        def _():
            up_copy(j).wait_send()

        @pl.when(j < z)
        def _():
            down_copy(j).wait_send()

        return carry

    lax.fori_loop(0, depth, finish, 0)


def scatter_all(local, tiny, mesh):
    dp, fsdp = mesh.shape["dp"], mesh.shape["fsdp"]
    _, total, width = local.shape
    rows = total // (dp * fsdp)
    if fsdp != 2 or dp % 4:
        shard = lax.psum_scatter(
            local.reshape(BLOCKS, dp * fsdp, rows, width),
            ("dp", "fsdp"),
            scatter_dimension=1,
            tiled=False,
        )
        return shard.astype(jnp.float32), lax.psum(tiny, ("dp", "fsdp"))
    depth = dp // 4
    dma = pltpu.SemaphoreType.DMA
    bf16 = jnp.bfloat16
    return pl.pallas_call(
        functools.partial(scatter_kernel, depth),
        out_shape=(
            jax.ShapeDtypeStruct((BLOCKS, rows, width), jnp.float32),
            jax.ShapeDtypeStruct((8, 128), jnp.float32),
        ),
        in_specs=[pl.BlockSpec(memory_space=pl.ANY), pl.BlockSpec(memory_space=pltpu.VMEM)],
        out_specs=(
            pl.BlockSpec(memory_space=pltpu.VMEM),
            pl.BlockSpec(memory_space=pltpu.VMEM),
        ),
        scratch_shapes=[
            pltpu.VMEM((depth, BLOCKS, 2, 2, rows, width), bf16),
            pltpu.VMEM((depth, BLOCKS, 2, 2, rows, width), bf16),
            pltpu.VMEM((depth, HALF, 2, rows, width), bf16),
            pltpu.VMEM((depth, HALF, 2, rows, width), bf16),
            pltpu.VMEM((depth, HALF, rows, width), bf16),
            pltpu.VMEM((depth, HALF, rows, width), bf16),
            pltpu.VMEM((depth, BLOCKS, rows, width), bf16),
            pltpu.VMEM((depth, BLOCKS, rows, width), bf16),
            pltpu.VMEM((4, 8, 128), jnp.float32),
            pltpu.VMEM((3 + depth, 8, 128), jnp.float32),
            dma((depth,)),
            dma((depth,)),
            dma((depth,)),
            dma((4, depth)),
            dma((4, depth)),
            dma((depth,)),
            dma((2, depth)),
            dma((1 + 2 * depth,)),
            dma((3 + depth,)),
        ],
        compiler_params=pltpu.CompilerParams(
            collective_id=1, has_side_effects=True, vmem_limit_bytes=60 * 1024 * 1024
        ),
        name="scatter_all",
    )(local.reshape(BLOCKS, depth, 2, 2, 2, rows, width), tiny)


W = D // G
F32, BF16 = jnp.float32, jnp.bfloat16
PAD = 8


def nn(a, b):
    return lax.dot_general(a, b, (((1,), (0,)), ((), ())), preferred_element_type=F32)


def nt(a, b):
    return lax.dot_general(a, b, (((1,), (1,)), ((), ())), preferred_element_type=F32)


def tn(a, b):
    return lax.dot_general(a, b, (((0,), (0,)), ((), ())), preferred_element_type=F32)


def spread(rows):
    head = lax.broadcasted_iota(jnp.int32, (rows, W), 0) % 8
    channel = lax.broadcasted_iota(jnp.int32, (rows, W), 1) // HD
    return (head == channel).astype(F32).astype(BF16)


def forward_kernel(
    len_ref,
    hid_ref,
    win_ref,
    wpt_ref,
    depth_ref,
    kmt_ref,
    x_ref,
    proj_ref,
    dl_ref,
    kc_ref,
    wt_ref,
    lse_ref,
    ctx_ref,
    xs,
    sv,
    ot,
):
    length = len_ref[pl.program_id(0)]
    inside = lax.broadcasted_iota(jnp.int32, (SEQ, 1), 0) < length
    x = jnp.where(inside, hid_ref[0], jnp.zeros((), BF16))
    x_ref[0] = x
    xs[0:PAD] = jnp.zeros((PAD, D), F32)
    xs[PAD + SEQ :] = jnp.zeros((PAD, D), F32)
    xs[PAD : PAD + SEQ] = x.astype(F32)
    sv[0:PAD] = jnp.zeros((PAD, W), F32)
    sv[PAD + SEQ :] = jnp.zeros((PAD, W), F32)

    for b in range(4):
        part = nn(x_ref[0], win_ref[b]).astype(BF16)
        proj_ref[0, :, b * W : (b + 1) * W] = part
        if b == 3:
            sv[PAD : PAD + SEQ] = part.astype(F32)

    def column(c, carry):
        lane = pl.ds(pl.multiple_of(c * 128, 128), 128)
        for r in range(8):
            total = jnp.zeros((64, 128), F32)
            for k in range(K):
                start = PAD + r * 64 + k - K // 2
                total = total + xs[start : start + 64, lane] * depth_ref[k : k + 1, lane]
            dl_ref[0, r * 64 : (r + 1) * 64, lane] = total.astype(BF16)
        return carry

    lax.fori_loop(0, D // 128, column, 0)
    kc_ref[0] = nn(dl_ref[0], wpt_ref[0])
    mk = (kc_ref[0] * proj_ref[0, :, 0:W].astype(F32)).astype(BF16)
    logits = nt(kmt_ref[...], mk)
    top = logits[0:8]
    for k in range(1, K):
        top = jnp.maximum(top, logits[k * 8 : k * 8 + 8])
    parts = [jnp.exp(logits[k * 8 : k * 8 + 8] - top) for k in range(K)]
    inverse = 1.0 / sum(parts)
    both = []
    for k in range(K):
        weight = parts[k] * inverse
        wt_ref[0, k * 8 : k * 8 + 8] = weight
        high = weight.astype(BF16).astype(F32)
        both.append(jnp.concatenate([high, weight - high], axis=0).astype(BF16))
    e16 = spread(16)
    for r in range(4):
        total = jnp.zeros((128, W), F32)
        for k in range(K):
            start = PAD + r * 128 + k - K // 2
            total = total + tn(both[k][:, r * 128 : (r + 1) * 128], e16) * sv[start : start + 128]
        ctx_ref[0, r * 128 : (r + 1) * 128, W:] = total.astype(BF16)

    lane_head = lax.broadcasted_iota(jnp.int32, (1, 128), 1) // HD
    bias = jnp.where(inside, 0.0, -1e30).astype(F32)

    def pair(p, carry):
        def slab(part):
            return proj_ref[0, :, pl.ds(pl.multiple_of(part * W + p * 128, 128), 128)]

        q2, k2, v2 = slab(0), slab(1), slab(2)
        for h in range(2):
            scale = jnp.where(lane_head == h, 1.0 / math.sqrt(HD), 0.0).astype(BF16)
            scores = nt(k2, q2 * scale) + bias
            peak = jnp.max(scores, axis=0, keepdims=True)
            power = jnp.exp(scores - peak)
            total = jnp.sum(power, axis=0, keepdims=True)
            lse_ref[0, pl.ds(p * 2 + h, 1)] = peak + jnp.log(total)
            probs = (power * (1.0 / total)).astype(BF16)
            ot[h * HD : (h + 1) * HD] = tn(v2, probs)[h * HD : (h + 1) * HD]
        ctx_ref[0, :, pl.ds(pl.multiple_of(p * 128, 128), 128)] = ot[...].T.astype(BF16)
        return carry

    lax.fori_loop(0, HEADS // 2, pair, 0)


def forward(lengths, hidden, full, depth, kmt):
    rows = hidden.shape[0]

    def per_row(*shape):
        return pl.BlockSpec((1,) + shape, lambda r: (r, 0, 0))

    def out(dtype, *shape):
        return jax.ShapeDtypeStruct((rows,) + shape, dtype)

    return pl.pallas_call(
        forward_kernel,
        grid=(rows,),
        out_shape=(
            out(BF16, SEQ, D),
            out(BF16, SEQ, 4 * W),
            out(BF16, SEQ, D),
            out(F32, SEQ, W),
            out(F32, 8 * K, SEQ),
            out(F32, 8, SEQ),
            out(BF16, SEQ, D),
        ),
        in_specs=[
            pl.BlockSpec(memory_space=pltpu.SMEM),
            per_row(SEQ, D),
            pl.BlockSpec((4, D, W), lambda r: (0, 0, 0)),
            pl.BlockSpec((1, D, W), lambda r: (14, 0, 0)),
            pl.BlockSpec((16, D), lambda r: (0, 0)),
            pl.BlockSpec((8 * K, W), lambda r: (0, 0)),
        ],
        out_specs=(
            per_row(SEQ, D),
            per_row(SEQ, 4 * W),
            per_row(SEQ, D),
            per_row(SEQ, W),
            per_row(8 * K, SEQ),
            per_row(8, SEQ),
            per_row(SEQ, D),
        ),
        scratch_shapes=[
            pltpu.VMEM((SEQ + 2 * PAD, D), F32),
            pltpu.VMEM((SEQ + 2 * PAD, W), F32),
            pltpu.VMEM((128, SEQ), F32),
        ],
        compiler_params=pltpu.CompilerParams(vmem_limit_bytes=56 * 1024 * 1024),
        name="mixer_forward",
    )(lengths, hidden, full, full, depth, kmt)


TILE = 256
CHUNK = 16


def ffn_kernel(
    len_ref,
    ctx_ref,
    x_ref,
    og_ref,
    wout_ref,
    wdn_ref,
    wup_ref,
    gb_ref,
    y_ref,
    act_ref,
    gpre_ref,
    fb_ref,
    gffn_ref,
    gmix_ref,
    gr1_ref,
    gctx_ref,
    stat_ref,
    mix,
    first,
    n1,
    inv,
    ffn,
    pre,
    dg,
    gr2,
):
    step = pl.program_id(0)
    row = step // (SEQ // TILE)
    base = (step % (SEQ // TILE)) * TILE
    left = len_ref[row] - base

    @pl.when(step == 0)
    def _():
        stat_ref[...] = jnp.zeros_like(stat_ref)

    for b in range(2):
        mix[:, b * W : (b + 1) * W] = nn(ctx_ref[...], wout_ref[b])

    def mask_of(i):
        return (lax.broadcasted_iota(jnp.int32, (CHUNK, 1), 0) + i * CHUNK < left).astype(F32)

    def fold(values):
        return jnp.sum(values.reshape(CHUNK // 8, 8, D), axis=0)

    def tally(k, values):
        stat_ref[k] = stat_ref[k] + fold(values)

    def rows_of(i):
        return pl.ds(pl.multiple_of(i * CHUNK, CHUNK), CHUNK)

    def norm(values):
        average = jnp.mean(values, axis=-1, keepdims=True)
        centered = values - average
        inverse = lax.rsqrt(jnp.mean(centered * centered, axis=-1, keepdims=True) + EPSILON)
        return centered * inverse, inverse

    def norm_back(grad, normed, inverse, gain):
        scaled = grad * gain
        mean = jnp.mean(scaled, axis=-1, keepdims=True)
        other = jnp.mean(scaled * normed, axis=-1, keepdims=True)
        return inverse * (scaled - mean - normed * other)

    def norm_one(i, carry):
        rows = rows_of(i)
        xf, mixed = x_ref[rows].astype(F32), mix[rows]
        normed, inverse = norm(xf + mixed)
        result = normed * gb_ref[0:1] + gb_ref[2:3]
        n1[rows] = normed
        inv[rows] = jnp.broadcast_to(inverse, (CHUNK, 128))
        first[rows] = result
        fb_ref[rows] = result.astype(BF16)
        tally(0, xf * xf)
        tally(1, mixed * mixed * mask_of(i))
        return carry

    lax.fori_loop(0, TILE // CHUNK, norm_one, 0)

    for s in range(4):
        g = s // 2
        pre[...] = nt(fb_ref[:, g * W : (g + 1) * W], wup_ref[s])

        def gelu(i, carry):
            rows = rows_of(i)
            v = pre[rows]
            phi = 0.5 + 0.5 * lax.erf(v * math.sqrt(0.5))
            act_ref[rows, s * D : (s + 1) * D] = (v * phi).astype(BF16)
            dg[s, rows] = phi + v * jnp.exp(v * v * -0.5) * (1.0 / math.sqrt(2.0 * math.pi))
            return carry

        lax.fori_loop(0, TILE // CHUNK, gelu, 0)
        part = nn(act_ref[:, s * D : (s + 1) * D], wdn_ref[s])
        lanes = slice(g * W, (g + 1) * W)
        if s % 2 == 0:
            ffn[:, lanes] = part
        else:
            ffn[:, lanes] += part

    def norm_two(i, carry):
        rows = rows_of(i)
        mask = mask_of(i)
        out = ffn[rows]
        normed, inverse = norm(first[rows] + out)
        y = (normed * gb_ref[1:2] + gb_ref[3:4]) * mask
        y_ref[rows] = y.astype(BF16)
        grad = og_ref[rows].astype(F32) * mask
        back = norm_back(grad, normed, inverse, gb_ref[1:2])
        gr2[rows] = back
        gffn_ref[rows] = back.astype(BF16)
        tally(2, out * out * mask)
        tally(3, y * y)
        tally(5, grad * normed)
        tally(7, grad)
        return carry

    lax.fori_loop(0, TILE // CHUNK, norm_two, 0)

    for s in range(4):
        g = s // 2
        lanes = slice(g * W, (g + 1) * W)
        pre[...] = nt(gffn_ref[:, lanes], wdn_ref[s])

        def times(i, carry):
            rows = rows_of(i)
            gpre_ref[rows, s * D : (s + 1) * D] = (pre[rows] * dg[s, rows]).astype(BF16)
            return carry

        lax.fori_loop(0, TILE // CHUNK, times, 0)
        gr2[:, lanes] += nn(gpre_ref[:, s * D : (s + 1) * D], wup_ref[s])

    def norm_one_back(i, carry):
        rows = rows_of(i)
        grad, normed = gr2[rows], n1[rows]
        back = norm_back(grad, normed, inv[rows, 0:1], gb_ref[0:1])
        gr1_ref[rows] = back
        gmix_ref[rows] = back.astype(BF16)
        tally(4, grad * normed)
        tally(6, grad)
        return carry

    lax.fori_loop(0, TILE // CHUNK, norm_one_back, 0)
    gctx_ref[...] = (
        nt(gmix_ref[:, 0:W], wout_ref[0]) + nt(gmix_ref[:, W:], wout_ref[1])
    ).astype(BF16)


def feed_forward(lengths, ctx, x, out_grad, full, gb):
    tokens = x.shape[0]

    def per_tile(width):
        return pl.BlockSpec((TILE, width), lambda i: (i, 0))

    def out(dtype, width):
        return jax.ShapeDtypeStruct((tokens, width), dtype)

    return pl.pallas_call(
        ffn_kernel,
        grid=(tokens // TILE,),
        out_shape=(
            out(BF16, D),
            out(BF16, 4 * D),
            out(BF16, 4 * D),
            out(BF16, D),
            out(BF16, D),
            out(BF16, D),
            out(F32, D),
            out(BF16, D),
            jax.ShapeDtypeStruct((8, 8, D), F32),
        ),
        in_specs=[
            pl.BlockSpec(memory_space=pltpu.SMEM),
            per_tile(D),
            per_tile(D),
            per_tile(D),
            pl.BlockSpec((2, D, W), lambda i: (6, 0, 0)),
            pl.BlockSpec((4, D, W), lambda i: (1, 0, 0)),
            pl.BlockSpec((4, D, W), lambda i: (2, 0, 0)),
            pl.BlockSpec((8, D), lambda i: (0, 0)),
        ],
        out_specs=(
            per_tile(D),
            per_tile(4 * D),
            per_tile(4 * D),
            per_tile(D),
            per_tile(D),
            per_tile(D),
            per_tile(D),
            per_tile(D),
            pl.BlockSpec((8, 8, D), lambda i: (0, 0, 0)),
        ),
        scratch_shapes=[
            pltpu.VMEM((TILE, D), F32),
            pltpu.VMEM((TILE, D), F32),
            pltpu.VMEM((TILE, D), F32),
            pltpu.VMEM((TILE, 128), F32),
            pltpu.VMEM((TILE, D), F32),
            pltpu.VMEM((TILE, D), F32),
            pltpu.VMEM((4, TILE, D), F32),
            pltpu.VMEM((TILE, D), F32),
        ],
        compiler_params=pltpu.CompilerParams(vmem_limit_bytes=56 * 1024 * 1024),
        name="feed_forward",
    )(lengths, ctx, x, out_grad, full, full, full, gb)


def backward_kernel(
    len_ref,
    x_ref,
    proj_ref,
    dl_ref,
    kc_ref,
    wt_ref,
    lse_ref,
    gctx_ref,
    gr1_ref,
    win_ref,
    wpt_ref,
    depth_ref,
    kmt_ref,
    gproj_ref,
    gkc_ref,
    gin_ref,
    gkm_ref,
    gdk_ref,
    sv,
    gc,
    xs,
    gd,
    gs,
    gq,
    gt,
    dqt,
):
    row = pl.program_id(0)
    length = len_ref[row]
    inside = lax.broadcasted_iota(jnp.int32, (SEQ, 1), 0) < length

    @pl.when(row == 0)
    def _():
        gkm_ref[...] = jnp.zeros_like(gkm_ref)
        gdk_ref[...] = jnp.zeros_like(gdk_ref)

    for ref, width in ((sv, W), (gc, W), (xs, D), (gd, D)):
        ref[0:PAD] = jnp.zeros((PAD, width), F32)
        ref[PAD + SEQ :] = jnp.zeros((PAD, width), F32)
    sv[PAD : PAD + SEQ] = proj_ref[0, :, 3 * W :].astype(F32)
    gc[PAD : PAD + SEQ] = gctx_ref[0, :, W:].astype(F32)
    xs[PAD : PAD + SEQ] = x_ref[0].astype(F32)

    e16 = spread(16)
    place_row = lax.broadcasted_iota(jnp.int32, (W, 128), 0) // HD
    place_col = lax.broadcasted_iota(jnp.int32, (W, 128), 1)
    both = []
    for k in range(K):
        weight = pltpu.roll(wt_ref[0, k * 8 : k * 8 + 8], (k - K // 2) % SEQ, 1)
        high = weight.astype(BF16).astype(F32)
        both.append(jnp.concatenate([high, weight - high], axis=0).astype(BF16))
    for r in range(4):
        rows = slice(r * 128, (r + 1) * 128)
        spans = jnp.zeros((128, 128), F32)
        total = jnp.zeros((128, W), F32)
        for k in range(K):
            start = PAD + r * 128 + k - K // 2
            product_k = gc[PAD + r * 128 : PAD + (r + 1) * 128] * sv[start : start + 128]
            chosen = (place_col == place_row + 8 * k).astype(F32).astype(BF16)
            spans = spans + nn(product_k.astype(BF16), chosen)
            start = PAD + r * 128 - k + K // 2
            total = total + tn(both[k][:, rows], e16) * gc[start : start + 128]
        gt[:, rows] = spans.T
        gproj_ref[0, rows, 3 * W :] = total.astype(BF16)
    center = jnp.zeros((8, SEQ), F32)
    for k in range(K):
        center = center + wt_ref[0, k * 8 : k * 8 + 8] * gt[k * 8 : k * 8 + 8]
    glt = jnp.concatenate(
        [
            wt_ref[0, k * 8 : k * 8 + 8] * (gt[k * 8 : k * 8 + 8] - center)
            for k in range(K)
        ],
        axis=0,
    ).astype(BF16)
    query = proj_ref[0, :, 0:W].astype(F32)
    mk = (kc_ref[0] * query).astype(BF16)
    gkm_ref[...] += nn(glt, mk)
    mixed = tn(glt, kmt_ref[...])
    gkc_ref[0] = (mixed * query).astype(BF16)
    gq[...] = mixed * kc_ref[0]
    gd[PAD : PAD + SEQ] = nt(gkc_ref[0], wpt_ref[0])

    def column(c, carry):
        lane = pl.ds(pl.multiple_of(c * 128, 128), 128)
        sums = [jnp.zeros((8, 128), F32)] * K
        for r in range(8):
            total = jnp.zeros((64, 128), F32)
            center = PAD + r * 64
            grad = gd[center : center + 64, lane]
            for k in range(K):
                start = center + k - K // 2
                sums[k] = sums[k] + jnp.sum(
                    (xs[start : start + 64, lane] * grad).reshape(8, 8, 128), axis=0
                )
                start = center - k + K // 2
                total = total + gd[start : start + 64, lane] * depth_ref[k : k + 1, lane]
            gs[r * 64 : (r + 1) * 64, lane] = total
        for k in range(K):
            gdk_ref[k, :, lane] = gdk_ref[k, :, lane] + sums[k]
        return carry

    lax.fori_loop(0, D // 128, column, 0)

    lane_head = lax.broadcasted_iota(jnp.int32, (1, 128), 1) // HD
    bias = jnp.where(inside, 0.0, -1e30).astype(F32)

    def pair(p, carry):
        def lanes(part):
            return pl.ds(pl.multiple_of(part * W + p * 128, 128), 128)

        q2, k2, v2 = (proj_ref[0, :, lanes(part)] for part in range(3))
        g2 = gctx_ref[0, :, lanes(0)]
        results = []
        for h in range(2):
            mine = lane_head == h
            scale = jnp.where(mine, 1.0 / math.sqrt(HD), 0.0).astype(BF16)
            scores = nt(k2, q2 * scale) + bias
            probs = jnp.exp(scores - lse_ref[0, pl.ds(p * 2 + h, 1)])
            grads = nt(v2 * jnp.where(mine, 1.0, 0.0).astype(BF16), g2)
            correction = jnp.sum(probs * grads, axis=0, keepdims=True)
            grad_scores = (probs * (grads - correction)).astype(BF16)
            dqt[h * HD : (h + 1) * HD] = tn(k2, grad_scores)[h * HD : (h + 1) * HD]
            results.append((nn(grad_scores, q2), nn(probs.astype(BF16), g2)))
        low = lane_head == 0
        scale = 1.0 / math.sqrt(HD)
        gproj_ref[0, :, lanes(0)] = (dqt[...].T * scale + gq[:, lanes(0)]).astype(BF16)
        gproj_ref[0, :, lanes(1)] = (jnp.where(low, results[0][0], results[1][0]) * scale).astype(BF16)
        gproj_ref[0, :, lanes(2)] = jnp.where(low, results[0][1], results[1][1]).astype(BF16)
        return carry

    lax.fori_loop(0, HEADS // 2, pair, 0)

    for b in range(4):
        gs[...] += nt(gproj_ref[0, :, b * W : (b + 1) * W], win_ref[b])
    gin_ref[0] = jnp.where(inside, gr1_ref[0] + gs[...], 0.0).astype(BF16)


def backward(lengths, x, proj, dl, kc, wt, lse, gctx, gr1, full, depth, kmt):
    rows = x.shape[0]

    def per_row(*shape):
        return pl.BlockSpec((1,) + shape, lambda r: (r, 0, 0))

    def out(dtype, *shape):
        return jax.ShapeDtypeStruct((rows,) + shape, dtype)

    return pl.pallas_call(
        backward_kernel,
        grid=(rows,),
        out_shape=(
            out(BF16, SEQ, 4 * W),
            out(BF16, SEQ, W),
            out(BF16, SEQ, D),
            jax.ShapeDtypeStruct((8 * K, W), F32),
            jax.ShapeDtypeStruct((K, 8, D), F32),
        ),
        in_specs=[
            pl.BlockSpec(memory_space=pltpu.SMEM),
            per_row(SEQ, D),
            per_row(SEQ, 4 * W),
            per_row(SEQ, D),
            per_row(SEQ, W),
            per_row(8 * K, SEQ),
            per_row(8, SEQ),
            per_row(SEQ, D),
            per_row(SEQ, D),
            pl.BlockSpec((4, D, W), lambda r: (0, 0, 0)),
            pl.BlockSpec((1, D, W), lambda r: (14, 0, 0)),
            pl.BlockSpec((16, D), lambda r: (0, 0)),
            pl.BlockSpec((8 * K, W), lambda r: (0, 0)),
        ],
        out_specs=(
            per_row(SEQ, 4 * W),
            per_row(SEQ, W),
            per_row(SEQ, D),
            pl.BlockSpec((8 * K, W), lambda r: (0, 0)),
            pl.BlockSpec((K, 8, D), lambda r: (0, 0, 0)),
        ),
        scratch_shapes=[
            pltpu.VMEM((SEQ + 2 * PAD, W), F32),
            pltpu.VMEM((SEQ + 2 * PAD, W), F32),
            pltpu.VMEM((SEQ + 2 * PAD, D), F32),
            pltpu.VMEM((SEQ + 2 * PAD, D), F32),
            pltpu.VMEM((SEQ, D), F32),
            pltpu.VMEM((SEQ, W), F32),
            pltpu.VMEM((128, SEQ), F32),
            pltpu.VMEM((128, SEQ), F32),
        ],
        compiler_params=pltpu.CompilerParams(vmem_limit_bytes=56 * 1024 * 1024),
        name="mixer_backward",
    )(lengths, x, proj, dl, kc, wt, lse, gctx, gr1, full, full, depth, kmt)


def pack(in_weight, depth_kernel, point_weight, kernel_weight, out_weight, up_weight, down_weight, norm_gains, norm_biases):
    rows = in_weight.shape[0]

    def halves(grouped):
        return grouped.reshape(G * 2, rows, W)

    kernel = kernel_weight.reshape(K, rows, 3).transpose(1, 0, 2).reshape(rows, 3 * K)
    small = jnp.concatenate([depth_kernel.T, kernel, norm_gains.T, norm_biases.T], axis=1)
    small = jnp.pad(small, ((0, 0), (0, W - small.shape[1])))
    return jnp.concatenate(
        [
            in_weight.reshape(rows, 4, W).transpose(1, 0, 2),
            halves(down_weight),
            halves(up_weight.transpose(0, 2, 1)),
            out_weight.reshape(rows, 2, W).transpose(1, 0, 2),
            point_weight[None],
            small[None],
        ],
        axis=0,
    )


def unpack(shard):
    rows = shard.shape[1]
    small = shard[15]
    kernel = small[:, K : 4 * K].reshape(rows, K, 3).transpose(1, 0, 2).reshape(K, 3 * rows)
    return (
        shard[0:4].transpose(1, 0, 2).reshape(rows, 4 * W),
        small[:, :K].T,
        shard[14],
        kernel,
        shard[12:14].transpose(1, 0, 2).reshape(rows, 2 * W),
        shard[8:12].reshape(G, 2 * rows, W).transpose(0, 2, 1),
        shard[4:8].reshape(G, 2 * rows, W),
        small[:, 4 * K : 4 * K + 2].T,
        small[:, 4 * K + 2 : 4 * K + 4].T,
    )


def layer(hidden, lengths, full, out_grad):
    rows = hidden.shape[0]
    tokens = rows * SEQ
    small = full[15].astype(F32)
    depth = jnp.pad(small[:, :K].T, ((0, 16 - K), (0, 0)))
    kernel = small[:, K : 4 * K].reshape(D, K, 3).transpose(1, 0, 2).reshape(K, W, HEADS)
    kmt = jnp.pad(kernel.transpose(0, 2, 1), ((0, 0), (0, 8 - HEADS), (0, 0)))
    kmt = kmt.reshape(8 * K, W).astype(BF16)
    gb = jnp.pad(small[:, 4 * K : 4 * K + 4].T, ((0, 4), (0, 0)))

    x, proj, dl, kc, wt, lse, ctx = forward(lengths, hidden, full, depth, kmt)
    flat_x, flat_ctx = x.reshape(tokens, D), ctx.reshape(tokens, D)
    y, act, gpre, fb, gffn, gmix, gr1, gctx, stat = feed_forward(
        lengths, flat_ctx, flat_x, out_grad.reshape(tokens, D), full, gb
    )
    gproj, gkc, gin, gkm, gdk = backward(
        lengths,
        x,
        proj,
        dl,
        kc,
        wt,
        lse,
        gctx.reshape(rows, SEQ, D),
        gr1.reshape(rows, SEQ, D),
        full,
        depth,
        kmt,
    )
    stat = jnp.sum(stat, axis=1)
    grad_kernel = gkm.reshape(K, 8, W)[:, :HEADS].transpose(0, 2, 1).reshape(K, D, 3)
    grad_small = jnp.concatenate(
        [
            jnp.sum(gdk, axis=1).T,
            grad_kernel.transpose(1, 0, 2).reshape(D, 3 * K),
            stat[4:8].T,
        ],
        axis=1,
    )
    grad_small = jnp.pad(grad_small, ((0, 0), (0, W - grad_small.shape[1]))).astype(BF16)
    local = weight_grads(flat_x, dl, gproj, gkc, flat_ctx, gmix, act, gffn, gpre, fb, grad_small)
    sums = jnp.sum(stat[0:4], axis=1)
    count = jnp.sum(lengths).astype(F32)
    tiny = jnp.pad(jnp.concatenate([sums, count[None]]), (0, 123))
    tiny = jnp.broadcast_to(tiny[None], (8, 128))
    return y.reshape(rows, SEQ, D), gin, local, tiny


def weight_grads(x, dl, gproj, gkc, ctx, gmix, act, gffn, gpre, fb, grad_small):
    tokens = x.shape[0]
    gproj, gkc, dl = gproj.reshape(tokens, 4 * W), gkc.reshape(tokens, W), dl.reshape(tokens, D)

    def block(a, b):
        return tn(a, b).astype(BF16)

    def group(values, g):
        return values[:, g * W : (g + 1) * W]

    blocks = [block(x, group(gproj, b)) for b in range(4)]
    blocks += [block(act[:, s * D : (s + 1) * D], group(gffn, s // 2)) for s in range(4)]
    blocks += [block(gpre[:, s * D : (s + 1) * D], group(fb, s // 2)) for s in range(4)]
    blocks += [block(ctx, group(gmix, b)) for b in range(2)]
    blocks += [block(dl, gkc), grad_small]
    return jnp.stack(blocks)


def body(
    mesh,
    hidden,
    lengths,
    in_weight,
    depth_kernel,
    point_weight,
    kernel_weight,
    out_weight,
    up_weight,
    down_weight,
    norm_gains,
    norm_biases,
    out_grad,
):
    full = gather_all(
        pack(
            in_weight,
            depth_kernel,
            point_weight,
            kernel_weight,
            out_weight,
            up_weight,
            down_weight,
            norm_gains,
            norm_biases,
        ),
        mesh,
    )
    output, input_grad, local, tiny = layer(hidden, lengths, full, out_grad)
    shard, totals = scatter_all(local, tiny, mesh)
    rms = jnp.sqrt(totals[0, :4] / (totals[0, 4] * D))
    return (output, input_grad) + unpack(shard) + (rms,)


def solution(mesh):
    in_specs = (
        P(("dp", "fsdp"), None, None),
        P(("dp", "fsdp")),
        P(("dp", "fsdp"), None),
        P(None, ("dp", "fsdp")),
        P(("dp", "fsdp"), None),
        P(None, ("dp", "fsdp")),
        P(("dp", "fsdp"), None),
        P(None, None, ("dp", "fsdp")),
        P(None, ("dp", "fsdp"), None),
        P(None, ("dp", "fsdp")),
        P(None, ("dp", "fsdp")),
        P(("dp", "fsdp"), None, None),
    )
    out_specs = (
        P(("dp", "fsdp"), None, None),
        P(("dp", "fsdp"), None, None),
        P(("dp", "fsdp"), None),
        P(None, ("dp", "fsdp")),
        P(("dp", "fsdp"), None),
        P(None, ("dp", "fsdp")),
        P(("dp", "fsdp"), None),
        P(None, None, ("dp", "fsdp")),
        P(None, ("dp", "fsdp"), None),
        P(None, ("dp", "fsdp")),
        P(None, ("dp", "fsdp")),
        P(),
    )
    return jax.shard_map(functools.partial(body, mesh), mesh=mesh, in_specs=in_specs, out_specs=out_specs, check_vma=False)
```

profile of v0, /device:TPU:0, one launch (start us, length us, event | category | flops | bytes accessed | tf_op | source)
XLA Modules:
  0.0 332.3 jit_solution(7136228657104761063)
XLA Ops:
  0.6 1.3 reduce_sum.39
  5.9 0.9 fusion.55
  7.7 0.9 constant_dynamic-update-slice_fusion.3
  10.9 54.8 %gather_all.1 = bf16[16,4,2,2,2,24,384]{6,5,4,3,2,1,0:T(8,128)(2,1)} custom-call(bf16[16,24,384]{2,1,0:T(8,128)(2,1)} %copy-done.15), custom_call_target="tpu_custom_call" | custom-call | tf_op jit(solution)/shard_map/gather_all/pallas_call | solution.py:190
  65.7 1.1 slice.119
  71.1 24.2 %mixer_forward.1 = (bf16[2,512,768]{2,1,0:T(8,128)(2,1)}, bf16[2,512,1536]{2,1,0:T(8,128)(2,1)}, bf16[2,512,768]{2,1,0:T(8,128)(2,1)}, f32[2,512,384]{2,1,0:T(8,...) custom-call(s32[2]{0:T(128)} %len_ref.5, bf16[2,512,768]{2,1,0:T(8,128)(2,1)} %hid_ref.1, ...), custom_call_target="tpu_custom_call" | custom-call | tf_op jit(solution)/shard_map/mixer_forward/pallas_call | solution.py:667
  95.3 76.8 %feed_forward.1 = (bf16[1024,768]{1,0:T(8,128)(2,1)}, bf16[1024,3072]{1,0:T(8,128)(2,1)}, bf16[1024,3072]{1,0:T(8,128)(2,1)}, bf16[1024,768]{1,0:T(8,128)(2,1)},...) custom-call(s32[2]{0:T(128)} %len_ref.5, ...), custom_call_target="tpu_custom_call" | custom-call | tf_op jit(solution)/shard_map/feed_forward/pallas_call | solution.py:865
  172.1 38.0 %mixer_backward.1 = (bf16[2,512,1536]{2,1,0:T(8,128)(2,1)}, bf16[2,512,384]{2,1,0:T(8,128)(2,1)}, bf16[2,512,768]{2,1,0:T(8,128)(2,1)}, f32[72,384]{1,0:T(8,128)}, f32[9,8,768]{2,1,0:T(8,128)}) custom-call(s32[2]{0:T(128)} %len_ref.5, bf16[2,512,768]{2,1,0:T(8,128)(2,1)} %get-tuple-element.36.x_ref, bf16[2,512,1536]{2,1,0:T(8,128)(2,1)} %get-tuple-element.38.proj_ref, ...), custom_call_target="tpu_custom_call" | custom-call | tf_op jit(solution)/shard_map/mixer_backward/pallas_call | solution.py:1062
  210.2 2.3 fusion.40
  213.5 3.1 convolution_convert_fusion.2
  216.6 1.8 convolution_convert_fusion.3
  218.4 1.8 convolution_convert_fusion.4
  220.3 1.8 convolution_convert_fusion.5
  222.1 1.0 convolution_convert_fusion
  223.2 1.0 convolution_convert_fusion.1
  224.8 1.9 fusion.25
  226.7 1.8 fusion.22
  228.5 1.8 fusion.19
  230.3 1.9 fusion.16
  232.2 1.8 fusion.37
  234.1 1.9 fusion.34
  235.9 1.9 fusion.31
  237.8 1.8 fusion.28
  242.5 0.9 constant_dynamic-update-slice_fusion.20
  249.6 0.9 constant_dynamic-update-slice_fusion.12
  254.1 0.9 constant_dynamic-update-slice_fusion.7
  255.0 0.9 constant_dynamic-update-slice_fusion.6
  256.8 64.0 %scatter_all.1 = (f32[16,24,384]{2,1,0:T(8,128)}, f32[8,128]{1,0:T(8,128)}) custom-call(bf16[16,4,2,2,2,24,384]{6,5,4,3,2,1,0:T(8,128)(2,1)} %constant_dynamic-update-slice_fusion.5.l_ref, f32[8,128]{1,0:T(8,128)} %broadcast_in_dim.18.t_ref), custom_call_target="tpu_custom_call" | custom-call | tf_op jit(solution)/shard_map/scatter_all/pallas_call | solution.py:506
  320.8 1.3 slice.155
  322.7 1.2 sqrt_bitcast_fusion
  325.5 1.4 slice_bitcast_fusion.3
  326.9 1.8 fusion.66
  (121 shorter events, 31.0 us)
Async XLA Ops:
  10.2 0.7 copy-start.15
  172.1 38.1 %copy-start.2 = (bf16[2,512,768]{2,1,0:T(8,128)(2,1)S(1)}, bf16[2,512,768]{2,1,0:T(8,128)(2,1)}, u32[]{:S(2)}) copy-start(bf16[2,512,768]{2,1,0:T(8,128)(2,1)} %get-tuple-element.39.dl_ref) | copy-start | bytes 4718596
  210.1 2.3 copy-start.17
  210.2 2.4 copy-start.16
  210.2 3.3 copy-start.18
  210.2 3.3 copy-start
  213.5 3.1 copy-start.19
  220.3 1.8 copy-start.1
  220.3 1.9 copy-start.22
  220.3 3.9 %slice-start.2 = ((s8[6291456]{0:T(1024)(128)(4,1)}), s8[4194304]{0:T(1024)(128)(4,1)S(1)}, s32[]{:S(2)}) async-start(s8[6291456]{0:T(1024)(128)(4,1)} %bitcast.187), calls=%async_computation.2 | async-start | bytes 8388608
  222.1 2.2 slice-start.3
  223.1 1.7 copy-start.21
  226.7 5.5 %slice-start = ((s8[6291456]{0:T(1024)(128)(4,1)}), s8[4194304]{0:T(1024)(128)(4,1)S(1)}, s32[]{:S(2)}) async-start(s8[6291456]{0:T(1024)(128)(4,1)} %bitcast.185), calls=%async_computation | async-start | bytes 8388608
  228.5 3.7 %slice-start.1 = ((s8[6291456]{0:T(1024)(128)(4,1)}), s8[2097152]{0:T(1024)(128)(4,1)S(1)}, s32[]{:S(2)}) async-start(s8[6291456]{0:T(1024)(128)(4,1)} %bitcast.185), calls=%async_computation.1 | async-start | bytes 4194304
  230.3 1.9 copy-start.20
  241.4 1.1 copy-start.14
  241.4 2.0 copy-start.12
  241.7 2.6 copy-start.9
  242.5 2.7 copy-start.6
  243.4 2.7 copy-start.13
  244.3 2.7 copy-start.11
  245.2 2.7 copy-start.8
  246.1 2.6 copy-start.5
  247.0 2.6 copy-start.10
  247.8 2.7 copy-start.7
  248.7 2.7 copy-start.4
  249.6 2.7 copy-start.3
where the time goes:
time: 333 us; the launch traced here: 332 us
  Pallas kernels  258 us (77%)
  local copies, waits for them, and re-layouts  41.5 us (12%)
  matrix products  27.7 us (8%)
    pallas_call x1, Pallas kernels, feed_forward(): pl.pallas_call(ffn_kernel, grid=(tokens // TILE,), out_shape=(out(BF16, D...  76.8 us
    pallas_call x1, Pallas kernels, scatter_all(): pl.pallas_call(functools.partial(scatter_kernel, depth), out_shape=(jax.S...  64 us
    pallas_call x1, Pallas kernels, gather_all(): pl.pallas_call(functools.partial(gather_kernel, depth), out_shape=jax.Sha...  54.8 us
    pallas_call x1, Pallas kernels, backward(): pl.pallas_call(backward_kernel, grid=(rows,), out_shape=(out(BF16, SEQ, 4...  38 us
    dot_general x15, matrix products, tn(): lax.dot_general(a, b, (((0,), (0,)), ((), ())), preferred_element_type=F32)  27.7 us
    unnamed x86, local copies, waits for them, and re-layouts  27.6 us
    pallas_call x1, Pallas kernels, forward(): pl.pallas_call(forward_kernel, grid=(rows,), out_shape=(out(BF16, SEQ, D)...  24.2 us

commit v1 on v0

--- a/solution.py
+++ b/solution.py
@@ -211,337 +211,6 @@
     return full.reshape(BLOCKS, dp * fsdp * rows, width)
 
 
-def scatter_kernel(
-    depth,
-    l_ref,
-    t_ref,
-    o_ref,
-    u_ref,
-    acc,
-    rc,
-    ry1,
-    rx1,
-    rx2,
-    ry2,
-    rup,
-    rdn,
-    tiny,
-    got,
-    load_sem,
-    cs,
-    cr,
-    ss,
-    sr,
-    zs,
-    zr,
-    ts,
-    tr,
-):
-    dp, z, x, core, y = place()
-    c_dev, x_dev, y_dev = partners(dp, x, core, y)
-    up_dev, down_dev = (dp + 4, y), (dp - 4, y)
-    steps = 2 * depth - 1
-    bf16, f32 = jnp.bfloat16, jnp.float32
-
-    def target(q):
-        return z + (depth - 1 - q // 2) * (1 - 2 * (q % 2))
-
-    def valid(q):
-        j = target(q)
-        return (q >= 0) & (q < steps) & (j >= 0) & (j < depth)
-
-    def load(j):
-        return pltpu.make_async_copy(l_ref.at[:, j, :, core, :], acc.at[j], load_sem.at[j])
-
-    def c_copy(j):
-        return send(l_ref.at[:, j, :, 1 - core, :], rc.at[j], cs.at[j], cr.at[j], c_dev)
-
-    def y1_copy(j):
-        return send(acc.at[j, pl.ds(0, HALF), :, 1 - y], ry1.at[j], ss.at[0, j], sr.at[0, j], y_dev)
-
-    def x1_copy(j):
-        return send(acc.at[j, pl.ds(HALF, HALF), 1 - x], rx1.at[j], ss.at[1, j], sr.at[1, j], x_dev)
-
-    def x2_copy(j):
-        return send(acc.at[j, pl.ds(0, HALF), 1 - x, y], rx2.at[j], ss.at[2, j], sr.at[2, j], x_dev)
-
-    def y2_copy(j):
-        return send(acc.at[j, pl.ds(HALF, HALF), x, 1 - y], ry2.at[j], ss.at[3, j], sr.at[3, j], y_dev)
-
-    def up_copy(j):
-        return send(acc.at[j, :, x, y], rup.at[j], zs.at[j], zr.at[0, j], up_dev)
-
-    def down_copy(j):
-        return send(acc.at[j, :, x, y], rdn.at[j], zs.at[j], zr.at[1, j], down_dev)
-
-    def issue(q, carry):
-        @pl.when(valid(q))
-        def _():
-            load(target(q)).start()
-
-        return carry
-
-    lax.fori_loop(0, steps, issue, 0)
-    lines = tuple((z >= d, (dp - 4 * d, y)) for d in range(1, depth)) + tuple(
-        (z + d < depth, (dp + 4 * d, y)) for d in range(1, depth)
-    )
-    meet((c_dev, x_dev, y_dev), lines)
-
-    def issue_core(q, carry):
-        @pl.when(valid(q))
-        def _():
-            c_copy(target(q)).start()
-
-        return carry
-
-    lax.fori_loop(0, steps, issue_core, 0)
-
-    tiny[0] = t_ref[...]
-
-    def t_copy(k):
-        return send(tiny.at[k], got.at[k], ts.at[k], tr.at[k], (c_dev, x_dev, y_dev)[k])
-
-    def t_line(d, way):
-        return send(
-            tiny.at[3],
-            got.at[3 + z],
-            ts.at[2 + d if way > 0 else 1 + depth + d],
-            tr.at[3 + z],
-            (dp + 4 * d * way, y),
-        )
-
-    def t_arrival(level):
-        return send(tiny.at[3], got.at[3 + level], ts.at[0], tr.at[3 + level], c_dev)
-
-    t_copy(0).start()
-
-    def add(into, other):
-        return (into.astype(f32) + other.astype(f32)).astype(bf16)
-
-    def first(j):
-        load(j).wait()
-        c_copy(j).wait_recv()
-
-        def block(b, carry):
-            acc[j, b] = add(acc[j, b], rc[j, b])
-            return carry
-
-        lax.fori_loop(0, BLOCKS, block, 0)
-        y1_copy(j).start()
-        x1_copy(j).start()
-
-    def second(j):
-        y1_copy(j).wait_recv()
-
-        def low(b, carry):
-            for a in range(2):
-                acc[j, b, a, y] = add(acc[j, b, a, y], ry1[j, b, a])
-            return carry
-
-        lax.fori_loop(0, HALF, low, 0)
-        x2_copy(j).start()
-        x1_copy(j).wait_recv()
-
-        def high(b, carry):
-            for a in range(2):
-                acc[j, HALF + b, x, a] = add(acc[j, HALF + b, x, a], rx1[j, b, a])
-            return carry
-
-        lax.fori_loop(0, HALF, high, 0)
-        y2_copy(j).start()
-
-    def third(j):
-        x2_copy(j).wait_recv()
-        y2_copy(j).wait_recv()
-
-        @pl.when((j >= z) & (z > 0))
-        def _():
-            up_copy(j).wait_recv()
-
-        @pl.when((j <= z) & (z + 1 < depth))
-        def _():
-            down_copy(j).wait_recv()
-
-        def block(b, carry):
-            for part, other in ((0, rx2), (HALF, ry2)):
-                total = acc[j, part + b, x, y].astype(f32) + other[j, b].astype(f32)
-
-                @pl.when(j == z)
-                def _():
-                    o_ref[part + b] = total
-
-                @pl.when(j != z)
-                def _():
-                    acc[j, part + b, x, y] = total.astype(bf16)
-
-            return carry
-
-        lax.fori_loop(0, HALF, block, 0)
-
-        def more(ref, low_precision):
-            def block(b, carry):
-                if low_precision:
-                    acc[j, b, x, y] = add(acc[j, b, x, y], ref[j, b])
-                else:
-                    o_ref[b] = o_ref[b] + ref[j, b].astype(f32)
-                return carry
-
-            lax.fori_loop(0, BLOCKS, block, 0)
-
-        @pl.when((j > z) & (z > 0))
-        def _():
-            more(rup, True)
-
-        @pl.when((j < z) & (z + 1 < depth))
-        def _():
-            more(rdn, True)
-
-        @pl.when((j == z) & (z > 0))
-        def _():
-            more(rup, False)
-
-        @pl.when((j == z) & (z + 1 < depth))
-        def _():
-            more(rdn, False)
-
-        @pl.when(j > z)
-        def _():
-            up_copy(j).start()
-
-        @pl.when(j < z)
-        def _():
-            down_copy(j).start()
-
-    def stage(q, work):
-        @pl.when(valid(q))
-        def _():
-            work(target(q))
-
-    def step(q, carry):
-        stage(q, first)
-        stage(q - 1, second)
-        stage(q - 2, third)
-        return carry
-
-    lax.fori_loop(0, steps + 2, step, 0)
-
-    for k in range(3):
-        t_copy(k).wait_recv()
-        tiny[k + 1] = tiny[k] + got[k]
-        if k < 2:
-            t_copy(k + 1).start()
-    for d in range(1, depth):
-
-        @pl.when(z + d < depth)
-        def _():
-            t_line(d, 1).start()
-
-        @pl.when(z >= d)
-        def _():
-            t_line(d, -1).start()
-
-    for level in range(depth):
-
-        @pl.when(z == level)
-        def _():
-            got[3 + level] = tiny[3]
-
-        @pl.when(z != level)
-        def _():
-            t_arrival(level).wait_recv()
-
-    total = got[3]
-    for level in range(1, depth):
-        total = total + got[3 + level]
-    u_ref[...] = total
-
-    for d in range(1, depth):
-
-        @pl.when(z + d < depth)
-        def _():
-            t_line(d, 1).wait_send()
-
-        @pl.when(z >= d)
-        def _():
-            t_line(d, -1).wait_send()
-
-    for k in range(3):
-        t_copy(k).wait_send()
-
-    def finish(j, carry):
-        c_copy(j).wait_send()
-        y1_copy(j).wait_send()
-        x1_copy(j).wait_send()
-        x2_copy(j).wait_send()
-        y2_copy(j).wait_send()
-
-        @pl.when(j > z)
-        def _():
-            up_copy(j).wait_send()
-
-        @pl.when(j < z)
-        def _():
-            down_copy(j).wait_send()
-
-        return carry
-
-    lax.fori_loop(0, depth, finish, 0)
-
-
-def scatter_all(local, tiny, mesh):
-    dp, fsdp = mesh.shape["dp"], mesh.shape["fsdp"]
-    _, total, width = local.shape
-    rows = total // (dp * fsdp)
-    if fsdp != 2 or dp % 4:
-        shard = lax.psum_scatter(
-            local.reshape(BLOCKS, dp * fsdp, rows, width),
-            ("dp", "fsdp"),
-            scatter_dimension=1,
-            tiled=False,
-        )
-        return shard.astype(jnp.float32), lax.psum(tiny, ("dp", "fsdp"))
-    depth = dp // 4
-    dma = pltpu.SemaphoreType.DMA
-    bf16 = jnp.bfloat16
-    return pl.pallas_call(
-        functools.partial(scatter_kernel, depth),
-        out_shape=(
-            jax.ShapeDtypeStruct((BLOCKS, rows, width), jnp.float32),
-            jax.ShapeDtypeStruct((8, 128), jnp.float32),
-        ),
-        in_specs=[pl.BlockSpec(memory_space=pl.ANY), pl.BlockSpec(memory_space=pltpu.VMEM)],
-        out_specs=(
-            pl.BlockSpec(memory_space=pltpu.VMEM),
-            pl.BlockSpec(memory_space=pltpu.VMEM),
-        ),
-        scratch_shapes=[
-            pltpu.VMEM((depth, BLOCKS, 2, 2, rows, width), bf16),
-            pltpu.VMEM((depth, BLOCKS, 2, 2, rows, width), bf16),
-            pltpu.VMEM((depth, HALF, 2, rows, width), bf16),
-            pltpu.VMEM((depth, HALF, 2, rows, width), bf16),
-            pltpu.VMEM((depth, HALF, rows, width), bf16),
-            pltpu.VMEM((depth, HALF, rows, width), bf16),
-            pltpu.VMEM((depth, BLOCKS, rows, width), bf16),
-            pltpu.VMEM((depth, BLOCKS, rows, width), bf16),
-            pltpu.VMEM((4, 8, 128), jnp.float32),
-            pltpu.VMEM((3 + depth, 8, 128), jnp.float32),
-            dma((depth,)),
-            dma((depth,)),
-            dma((depth,)),
-            dma((4, depth)),
-            dma((4, depth)),
-            dma((depth,)),
-            dma((2, depth)),
-            dma((1 + 2 * depth,)),
-            dma((3 + depth,)),
-        ],
-        compiler_params=pltpu.CompilerParams(
-            collective_id=1, has_side_effects=True, vmem_limit_bytes=60 * 1024 * 1024
-        ),
-        name="scatter_all",
-    )(local.reshape(BLOCKS, depth, 2, 2, 2, rows, width), tiny)
-
-
 W = D // G
 F32, BF16 = jnp.float32, jnp.bfloat16
 PAD = 8
@@ -679,7 +348,7 @@
         in_specs=[
             pl.BlockSpec(memory_space=pltpu.SMEM),
             per_row(SEQ, D),
-            pl.BlockSpec((4, D, W), lambda r: (0, 0, 0)),
+            pl.BlockSpec((4, D, W), lambda r: (2, 0, 0)),
             pl.BlockSpec((1, D, W), lambda r: (14, 0, 0)),
             pl.BlockSpec((16, D), lambda r: (0, 0)),
             pl.BlockSpec((8 * K, W), lambda r: (0, 0)),
@@ -778,7 +447,8 @@
         n1[rows] = normed
         inv[rows] = jnp.broadcast_to(inverse, (CHUNK, 128))
         first[rows] = result
-        fb_ref[rows] = result.astype(BF16)
+        for g in range(G):
+            fb_ref[g, rows] = result[:, g * W : (g + 1) * W].astype(BF16)
         tally(0, xf * xf)
         tally(1, mixed * mixed * mask_of(i))
         return carry
@@ -787,18 +457,18 @@
 
     for s in range(4):
         g = s // 2
-        pre[...] = nt(fb_ref[:, g * W : (g + 1) * W], wup_ref[s])
+        pre[...] = nt(fb_ref[g], wup_ref[s])
 
         def gelu(i, carry):
             rows = rows_of(i)
             v = pre[rows]
             phi = 0.5 + 0.5 * lax.erf(v * math.sqrt(0.5))
-            act_ref[rows, s * D : (s + 1) * D] = (v * phi).astype(BF16)
+            act_ref[s, rows] = (v * phi).astype(BF16)
             dg[s, rows] = phi + v * jnp.exp(v * v * -0.5) * (1.0 / math.sqrt(2.0 * math.pi))
             return carry
 
         lax.fori_loop(0, TILE // CHUNK, gelu, 0)
-        part = nn(act_ref[:, s * D : (s + 1) * D], wdn_ref[s])
+        part = nn(act_ref[s], wdn_ref[s])
         lanes = slice(g * W, (g + 1) * W)
         if s % 2 == 0:
             ffn[:, lanes] = part
@@ -815,7 +485,8 @@
         grad = og_ref[rows].astype(F32) * mask
         back = norm_back(grad, normed, inverse, gb_ref[1:2])
         gr2[rows] = back
-        gffn_ref[rows] = back.astype(BF16)
+        for g in range(G):
+            gffn_ref[g, rows] = back[:, g * W : (g + 1) * W].astype(BF16)
         tally(2, out * out * mask)
         tally(3, y * y)
         tally(5, grad * normed)
@@ -827,29 +498,30 @@
     for s in range(4):
         g = s // 2
         lanes = slice(g * W, (g + 1) * W)
-        pre[...] = nt(gffn_ref[:, lanes], wdn_ref[s])
+        pre[...] = nt(gffn_ref[g], wdn_ref[s])
 
         def times(i, carry):
             rows = rows_of(i)
-            gpre_ref[rows, s * D : (s + 1) * D] = (pre[rows] * dg[s, rows]).astype(BF16)
+            gpre_ref[s, rows] = (pre[rows] * dg[s, rows]).astype(BF16)
             return carry
 
         lax.fori_loop(0, TILE // CHUNK, times, 0)
-        gr2[:, lanes] += nn(gpre_ref[:, s * D : (s + 1) * D], wup_ref[s])
+        gr2[:, lanes] += nn(gpre_ref[s], wup_ref[s])
 
     def norm_one_back(i, carry):
         rows = rows_of(i)
         grad, normed = gr2[rows], n1[rows]
         back = norm_back(grad, normed, inv[rows, 0:1], gb_ref[0:1])
         gr1_ref[rows] = back
-        gmix_ref[rows] = back.astype(BF16)
+        for g in range(2):
+            gmix_ref[g, rows] = back[:, g * W : (g + 1) * W].astype(BF16)
         tally(4, grad * normed)
         tally(6, grad)
         return carry
 
     lax.fori_loop(0, TILE // CHUNK, norm_one_back, 0)
     gctx_ref[...] = (
-        nt(gmix_ref[:, 0:W], wout_ref[0]) + nt(gmix_ref[:, W:], wout_ref[1])
+        nt(gmix_ref[0], wout_ref[0]) + nt(gmix_ref[1], wout_ref[1])
     ).astype(BF16)
 
 
@@ -861,17 +533,23 @@
 
     def out(dtype, width):
         return jax.ShapeDtypeStruct((tokens, width), dtype)
+
+    def slabs(count, width):
+        return pl.BlockSpec((count, TILE, width), lambda i: (0, i, 0))
+
+    def slabs_out(count, width):
+        return jax.ShapeDtypeStruct((count, tokens, width), BF16)
 
     return pl.pallas_call(
         ffn_kernel,
         grid=(tokens // TILE,),
         out_shape=(
             out(BF16, D),
-            out(BF16, 4 * D),
-            out(BF16, 4 * D),
-            out(BF16, D),
-            out(BF16, D),
-            out(BF16, D),
+            slabs_out(4, D),
+            slabs_out(4, D),
+            slabs_out(G, W),
+            slabs_out(G, W),
+            slabs_out(2, W),
             out(F32, D),
             out(BF16, D),
             jax.ShapeDtypeStruct((8, 8, D), F32),
@@ -882,17 +560,17 @@
             per_tile(D),
             per_tile(D),
             pl.BlockSpec((2, D, W), lambda i: (6, 0, 0)),
+            pl.BlockSpec((4, D, W), lambda i: (0, 0, 0)),
             pl.BlockSpec((4, D, W), lambda i: (1, 0, 0)),
-            pl.BlockSpec((4, D, W), lambda i: (2, 0, 0)),
             pl.BlockSpec((8, D), lambda i: (0, 0)),
         ],
         out_specs=(
             per_tile(D),
-            per_tile(4 * D),
-            per_tile(4 * D),
-            per_tile(D),
-            per_tile(D),
-            per_tile(D),
+            slabs(4, D),
+            slabs(4, D),
+            slabs(G, W),
+            slabs(G, W),
+            slabs(2, W),
             per_tile(D),
             per_tile(D),
             pl.BlockSpec((8, 8, D), lambda i: (0, 0, 0)),
@@ -976,7 +654,7 @@
             start = PAD + r * 128 - k + K // 2
             total = total + tn(both[k][:, rows], e16) * gc[start : start + 128]
         gt[:, rows] = spans.T
-        gproj_ref[0, rows, 3 * W :] = total.astype(BF16)
+        gproj_ref[3, rows] = total.astype(BF16)
     center = jnp.zeros((8, SEQ), F32)
     for k in range(K):
         center = center + wt_ref[0, k * 8 : k * 8 + 8] * gt[k * 8 : k * 8 + 8]
@@ -1039,14 +717,14 @@
         low = lane_head == 0
         scale = 1.0 / math.sqrt(HD)
         gproj_ref[0, :, lanes(0)] = (dqt[...].T * scale + gq[:, lanes(0)]).astype(BF16)
-        gproj_ref[0, :, lanes(1)] = (jnp.where(low, results[0][0], results[1][0]) * scale).astype(BF16)
-        gproj_ref[0, :, lanes(2)] = jnp.where(low, results[0][1], results[1][1]).astype(BF16)
+        gproj_ref[1, :, lanes(0)] = (jnp.where(low, results[0][0], results[1][0]) * scale).astype(BF16)
+        gproj_ref[2, :, lanes(0)] = jnp.where(low, results[0][1], results[1][1]).astype(BF16)
         return carry
 
     lax.fori_loop(0, HEADS // 2, pair, 0)
 
     for b in range(4):
-        gs[...] += nt(gproj_ref[0, :, b * W : (b + 1) * W], win_ref[b])
+        gs[...] += nt(gproj_ref[b], win_ref[b])
     gin_ref[0] = jnp.where(inside, gr1_ref[0] + gs[...], 0.0).astype(BF16)
 
 
@@ -1063,7 +741,7 @@
         backward_kernel,
         grid=(rows,),
         out_shape=(
-            out(BF16, SEQ, 4 * W),
+            jax.ShapeDtypeStruct((4, rows * SEQ, W), BF16),
             out(BF16, SEQ, W),
             out(BF16, SEQ, D),
             jax.ShapeDtypeStruct((8 * K, W), F32),
@@ -1079,13 +757,13 @@
             per_row(8, SEQ),
             per_row(SEQ, D),
             per_row(SEQ, D),
-            pl.BlockSpec((4, D, W), lambda r: (0, 0, 0)),
+            pl.BlockSpec((4, D, W), lambda r: (2, 0, 0)),
             pl.BlockSpec((1, D, W), lambda r: (14, 0, 0)),
             pl.BlockSpec((16, D), lambda r: (0, 0)),
             pl.BlockSpec((8 * K, W), lambda r: (0, 0)),
         ],
         out_specs=(
-            per_row(SEQ, 4 * W),
+            pl.BlockSpec((4, SEQ, W), lambda r: (0, r, 0)),
             per_row(SEQ, W),
             per_row(SEQ, D),
             pl.BlockSpec((8 * K, W), lambda r: (0, 0)),
@@ -1117,9 +795,9 @@
     small = jnp.pad(small, ((0, 0), (0, W - small.shape[1])))
     return jnp.concatenate(
         [
-            in_weight.reshape(rows, 4, W).transpose(1, 0, 2),
             halves(down_weight),
             halves(up_weight.transpose(0, 2, 1)),
+            in_weight.reshape(rows, 4, W).transpose(1, 0, 2),
             out_weight.reshape(rows, 2, W).transpose(1, 0, 2),
             point_weight[None],
             small[None],
@@ -1133,13 +811,13 @@
     small = shard[15]
     kernel = small[:, K : 4 * K].reshape(rows, K, 3).transpose(1, 0, 2).reshape(K, 3 * rows)
     return (
-        shard[0:4].transpose(1, 0, 2).reshape(rows, 4 * W),
+        shard[8:12].transpose(1, 0, 2).reshape(rows, 4 * W),
         small[:, :K].T,
         shard[14],
         kernel,
         shard[12:14].transpose(1, 0, 2).reshape(rows, 2 * W),
-        shard[8:12].reshape(G, 2 * rows, W).transpose(0, 2, 1),
-        shard[4:8].reshape(G, 2 * rows, W),
+        shard[4:8].reshape(G, 2 * rows, W).transpose(0, 2, 1),
+        shard[0:4].reshape(G, 2 * rows, W),
         small[:, 4 * K : 4 * K + 2].T,
         small[:, 4 * K + 2 : 4 * K + 4].T,
     )
@@ -1185,30 +863,366 @@
         axis=1,
     )
     grad_small = jnp.pad(grad_small, ((0, 0), (0, W - grad_small.shape[1]))).astype(BF16)
-    local = weight_grads(flat_x, dl, gproj, gkc, flat_ctx, gmix, act, gffn, gpre, fb, grad_small)
+    factors = (
+        flat_x,
+        dl.reshape(tokens, D),
+        gproj,
+        gkc.reshape(tokens, W),
+        flat_ctx,
+        gmix,
+        act,
+        gffn,
+        gpre,
+        fb,
+    )
     sums = jnp.sum(stat[0:4], axis=1)
     count = jnp.sum(lengths).astype(F32)
     tiny = jnp.pad(jnp.concatenate([sums, count[None]]), (0, 123))
     tiny = jnp.broadcast_to(tiny[None], (8, 128))
-    return y.reshape(rows, SEQ, D), gin, local, tiny
-
-
-def weight_grads(x, dl, gproj, gkc, ctx, gmix, act, gffn, gpre, fb, grad_small):
-    tokens = x.shape[0]
-    gproj, gkc, dl = gproj.reshape(tokens, 4 * W), gkc.reshape(tokens, W), dl.reshape(tokens, D)
-
-    def block(a, b):
-        return tn(a, b).astype(BF16)
-
-    def group(values, g):
-        return values[:, g * W : (g + 1) * W]
-
-    blocks = [block(x, group(gproj, b)) for b in range(4)]
-    blocks += [block(act[:, s * D : (s + 1) * D], group(gffn, s // 2)) for s in range(4)]
-    blocks += [block(gpre[:, s * D : (s + 1) * D], group(fb, s // 2)) for s in range(4)]
-    blocks += [block(ctx, group(gmix, b)) for b in range(2)]
-    blocks += [block(dl, gkc), grad_small]
-    return jnp.stack(blocks)
+    return y.reshape(rows, SEQ, D), gin, factors, grad_small, tiny
+
+
+def weight_grads(x, dl, gproj, gkc, ctx, gmix, act, gffn, gpre, fb, small):
+    pairs = [(act[s], gffn[s // 2]) for s in range(4)]
+    pairs += [(gpre[s], fb[s // 2]) for s in range(4)]
+    pairs += [(x, gproj[b]) for b in range(4)]
+    pairs += [(ctx, gmix[b]) for b in range(2)]
+    pairs += [(dl, gkc)]
+    return jnp.stack([tn(a, b).astype(BF16) for a, b in pairs] + [small])
+
+
+def scatter_kernel(
+    depth,
+    x_ref,
+    dl_ref,
+    gproj_ref,
+    gkc_ref,
+    ctx_ref,
+    gmix_ref,
+    act_ref,
+    gffn_ref,
+    gpre_ref,
+    fb_ref,
+    small_ref,
+    t_ref,
+    o_ref,
+    u_ref,
+    left,
+    right,
+    part,
+    rc,
+    r1,
+    r2,
+    ru,
+    rd,
+    tiny,
+    got,
+    left_sem,
+    right_sem,
+    cs,
+    cr,
+    s1,
+    q1,
+    s2,
+    q2,
+    us,
+    ur,
+    ds,
+    dr,
+    ts,
+    tr,
+):
+    dp, z, x, core, y = place()
+    c_dev, x_dev, y_dev = partners(dp, x, core, y)
+    up_dev, down_dev = (dp + 4, y), (dp - 4, y)
+    last = BLOCKS - 1
+
+    def fetch(t, act):
+        def both(a, b):
+            slot = t % 2
+            for copy in (
+                pltpu.make_async_copy(a, left.at[slot], left_sem.at[slot]),
+                pltpu.make_async_copy(b, right.at[slot], right_sem.at[slot]),
+            ):
+                act(copy)
+
+        @pl.when(t < 4)
+        def _():
+            both(act_ref.at[t], gffn_ref.at[t // 2])
+
+        @pl.when((t >= 4) & (t < 8))
+        def _():
+            both(gpre_ref.at[t - 4], fb_ref.at[(t - 4) // 2])
+
+        @pl.when((t >= 8) & (t < 12))
+        def _():
+            both(x_ref, gproj_ref.at[t - 8])
+
+        @pl.when((t >= 12) & (t < 14))
+        def _():
+            both(ctx_ref, gmix_ref.at[t - 12])
+
+        @pl.when(t == 14)
+        def _():
+            both(dl_ref, gkc_ref)
+
+    def c_copy(t):
+        return send(part.at[t, :, :, 1 - core], rc.at[t], cs.at[t], cr.at[t], c_dev)
+
+    def first_copy(t, by_y):
+        if by_y:
+            return send(part.at[t, :, :, core, 1 - y], r1.at[t], s1.at[t], q1.at[t], y_dev)
+        return send(part.at[t, :, 1 - x, core], r1.at[t], s1.at[t], q1.at[t], x_dev)
+
+    def second_copy(t, by_y):
+        if by_y:
+            return send(part.at[t, :, 1 - x, core, y], r2.at[t], s2.at[t], q2.at[t], x_dev)
+        return send(part.at[t, :, x, core, 1 - y], r2.at[t], s2.at[t], q2.at[t], y_dev)
+
+    def up_copy(t, bottom):
+        source = part.at[t, :, x, core, y] if bottom else ru.at[t]
+        return send(source, ru.at[t], us.at[t], ur.at[t], up_dev)
+
+    def down_copy(t, top):
+        source = part.at[t, :, x, core, y] if top else rd.at[t]
+        return send(source, rd.at[t], ds.at[t], dr.at[t], down_dev)
+
+    def t_copy(k):
+        return send(tiny.at[k], got.at[k], ts.at[k], tr.at[k], (c_dev, x_dev, y_dev)[k])
+
+    def t_line(d, way):
+        return send(
+            tiny.at[3],
+            got.at[3 + z],
+            ts.at[2 + d if way > 0 else 1 + depth + d],
+            tr.at[3 + z],
+            (dp + 4 * d * way, y),
+        )
+
+    def t_arrival(level):
+        return send(tiny.at[3], got.at[3 + level], ts.at[0], tr.at[3 + level], c_dev)
+
+    def add(into, other):
+        return (into.astype(F32) + other.astype(F32)).astype(BF16)
+
+    def parity(t, work):
+        @pl.when(t % 2 == 0)
+        def _():
+            work(True)
+
+        @pl.when(t % 2 == 1)
+        def _():
+            work(False)
+
+    fetch(0, lambda copy: copy.start())
+    lines = tuple((z >= d, (dp - 4 * d, y)) for d in range(1, depth)) + tuple(
+        (z + d < depth, (dp + 4 * d, y)) for d in range(1, depth)
+    )
+    meet((c_dev, x_dev, y_dev), lines)
+    tiny[0] = t_ref[...]
+    t_copy(0).start()
+
+    def multiply(t):
+        @pl.when(t + 1 < last)
+        def _():
+            fetch(t + 1, lambda copy: copy.start())
+
+        @pl.when(t < last)
+        def _():
+            fetch(t, lambda copy: copy.wait())
+            slot = t % 2
+            for c in range(2):
+                block = tn(left[slot, :, c * W : (c + 1) * W], right[slot])
+                half = depth // 2
+                part[t, c * half : (c + 1) * half] = block.reshape(
+                    (half,) + part.shape[2:]
+                ).astype(BF16)
+
+        @pl.when(t == last)
+        def _():
+            part[t] = small_ref[...]
+
+        c_copy(t).start()
+
+    def stage_core(t):
+        c_copy(t).wait_recv()
+
+        def level(j, carry):
+            part[t, j, :, core] = add(part[t, j, :, core], rc[t, j])
+            return carry
+
+        lax.fori_loop(0, depth, level, 0)
+        parity(t, lambda by_y: first_copy(t, by_y).start())
+
+    def stage_first(t):
+        def work(by_y):
+            first_copy(t, by_y).wait_recv()
+            if by_y:
+                part[t, :, :, core, y] = add(part[t, :, :, core, y], r1[t])
+            else:
+                part[t, :, x, core] = add(part[t, :, x, core], r1[t])
+            second_copy(t, by_y).start()
+
+        parity(t, work)
+
+    def stage_second(t):
+        parity(t, lambda by_y: second_copy(t, by_y).wait_recv())
+        part[t, :, x, core, y] = add(part[t, :, x, core, y], r2[t])
+        o_ref[t] = part[t, z, x, core, y].astype(F32)
+
+    def stage_up(t):
+        @pl.when(z == 0)
+        def _():
+            up_copy(t, True).start()
+
+        @pl.when(z > 0)
+        def _():
+            up_copy(t, False).wait_recv()
+            o_ref[t] = o_ref[t] + ru[t, z].astype(F32)
+
+        @pl.when((z > 0) & (z + 1 < depth))
+        def _():
+            ru[t] = add(ru[t], part[t, :, x, core, y])
+            up_copy(t, False).start()
+
+    def stage_down(t):
+        @pl.when(z + 1 == depth)
+        def _():
+            down_copy(t, True).start()
+
+        @pl.when(z + 1 < depth)
+        def _():
+            down_copy(t, False).wait_recv()
+            o_ref[t] = o_ref[t] + rd[t, z].astype(F32)
+
+        @pl.when((z > 0) & (z + 1 < depth))
+        def _():
+            rd[t] = add(rd[t], part[t, :, x, core, y])
+            down_copy(t, False).start()
+
+    def stage(t, work):
+        @pl.when((t >= 0) & (t < BLOCKS))
+        def _():
+            work(t)
+
+    def tick(t, carry):
+        stage(t, multiply)
+        stage(t - 1, stage_core)
+        stage(t - 3, stage_first)
+        stage(t - 5, stage_second)
+        stage(t - 5 - z, stage_up)
+        stage(t - 5 - (depth - 1 - z), stage_down)
+        return carry
+
+    lax.fori_loop(0, BLOCKS + 5 + depth, tick, 0)
+
+    for k in range(3):
+        t_copy(k).wait_recv()
+        tiny[k + 1] = tiny[k] + got[k]
+        if k < 2:
+            t_copy(k + 1).start()
+    for d in range(1, depth):
+
+        @pl.when(z + d < depth)
+        def _():
+            t_line(d, 1).start()
+
+        @pl.when(z >= d)
+        def _():
+            t_line(d, -1).start()
+
+    for level in range(depth):
+
+        @pl.when(z == level)
+        def _():
+            got[3 + level] = tiny[3]
+
+        @pl.when(z != level)
+        def _():
+            t_arrival(level).wait_recv()
+
+    total = got[3]
+    for level in range(1, depth):
+        total = total + got[3 + level]
+    u_ref[...] = total
+
+    for d in range(1, depth):
+
+        @pl.when(z + d < depth)
+        def _():
+            t_line(d, 1).wait_send()
+
+        @pl.when(z >= d)
+        def _():
+            t_line(d, -1).wait_send()
+
+    for k in range(3):
+        t_copy(k).wait_send()
+
+    def finish(t, carry):
+        c_copy(t).wait_send()
+        parity(t, lambda by_y: first_copy(t, by_y).wait_send())
+        parity(t, lambda by_y: second_copy(t, by_y).wait_send())
+
+        @pl.when(z + 1 < depth)
+        def _():
+            up_copy(t, False).wait_send()
+
+        @pl.when(z > 0)
+        def _():
+            down_copy(t, False).wait_send()
+
+        return carry
+
+    lax.fori_loop(0, BLOCKS, finish, 0)
+
+
+def scatter_all(factors, small, tiny, mesh):
+    dp, fsdp = mesh.shape["dp"], mesh.shape["fsdp"]
+    rows = D // (dp * fsdp)
+    if fsdp != 2 or dp % 4:
+        local = weight_grads(*factors, small)
+        shard = lax.psum_scatter(
+            local.reshape(BLOCKS, dp * fsdp, rows, W),
+            ("dp", "fsdp"),
+            scatter_dimension=1,
+            tiled=False,
+        )
+        return shard.astype(F32), lax.psum(tiny, ("dp", "fsdp"))
+    depth = dp // 4
+    tokens = factors[0].shape[0]
+    dma = pltpu.SemaphoreType.DMA
+    anywhere = pl.BlockSpec(memory_space=pl.ANY)
+    inside = pl.BlockSpec(memory_space=pltpu.VMEM)
+    return pl.pallas_call(
+        functools.partial(scatter_kernel, depth),
+        out_shape=(
+            jax.ShapeDtypeStruct((BLOCKS, rows, W), F32),
+            jax.ShapeDtypeStruct((8, 128), F32),
+        ),
+        in_specs=[anywhere] * len(factors) + [inside, inside],
+        out_specs=(inside, inside),
+        scratch_shapes=[
+            pltpu.VMEM((2, tokens, D), BF16),
+            pltpu.VMEM((2, tokens, W), BF16),
+            pltpu.VMEM((BLOCKS, depth, 2, 2, 2, rows, W), BF16),
+            pltpu.VMEM((BLOCKS, depth, 2, 2, rows, W), BF16),
+            pltpu.VMEM((BLOCKS, depth, 2, rows, W), BF16),
+            pltpu.VMEM((BLOCKS, depth, rows, W), BF16),
+            pltpu.VMEM((BLOCKS, depth, rows, W), BF16),
+            pltpu.VMEM((BLOCKS, depth, rows, W), BF16),
+            pltpu.VMEM((4, 8, 128), F32),
+            pltpu.VMEM((3 + depth, 8, 128), F32),
+            dma((2,)),
+            dma((2,)),
+        ]
+        + [dma((BLOCKS,))] * 10
+        + [dma((1 + 2 * depth,)), dma((3 + depth,))],
+        compiler_params=pltpu.CompilerParams(
+            collective_id=1, has_side_effects=True, vmem_limit_bytes=60 * 1024 * 1024
+        ),
+        name="scatter_all",
+    )(*factors, small.reshape(depth, 2, 2, 2, rows, W), tiny)
 
 
 def body(
@@ -1240,8 +1254,8 @@
         ),
         mesh,
     )
-    output, input_grad, local, tiny = layer(hidden, lengths, full, out_grad)
-    shard, totals = scatter_all(local, tiny, mesh)
+    output, input_grad, factors, small, tiny = layer(hidden, lengths, full, out_grad)
+    shard, totals = scatter_all(factors, small, tiny, mesh)
     rms = jnp.sqrt(totals[0, :4] / (totals[0, 4] * D))
     return (output, input_grad) + unpack(shard) + (rms,)
 

time: 333 us -> 311 us (0.934)
  matrix products: 27.7 us -> 0 us
  Pallas kernels: 258 us -> 278 us
  local copies, waits for them, and re-layouts: 41.5 us -> 26.4 us
    dot_general x15 -> x0, matrix products: 27.7 us -> none  [tn(): lax.dot_general(a, b, (((0,), (0,)), ((), ())), preferred_element_type=F32)]
    pallas_call x1, Pallas kernels: 64 us -> 83.7 us  [scatter_all(): pl.pallas_call(functools.partial(scatter_kernel, depth), out_shape=(jax.S...]
    unnamed x86 -> x25, local copies, waits for them, and re-layouts: 27.6 us -> 12.7 us
where the time goes in v1:
time: 311 us; the launch traced here: 310 us
  Pallas kernels  278 us (89%)
  local copies, waits for them, and re-layouts  26.4 us (8%)
  other arithmetic  3.25 us (1%)
    pallas_call x1, Pallas kernels, scatter_all(): pl.pallas_call(functools.partial(scatter_kernel, depth), out_shape=(jax.S...  83.7 us
    pallas_call x1, Pallas kernels, feed_forward(): pl.pallas_call(ffn_kernel, grid=(tokens // TILE,), out_shape=(out(BF16, D...  77.5 us
    pallas_call x1, Pallas kernels, gather_all(): pl.pallas_call(functools.partial(gather_kernel, depth), out_shape=jax.Sha...  54.8 us
    pallas_call x1, Pallas kernels, backward(): pl.pallas_call(backward_kernel, grid=(rows,), out_shape=(jax.ShapeDtypeSt...  38.2 us
    pallas_call x1, Pallas kernels, forward(): pl.pallas_call(forward_kernel, grid=(rows,), out_shape=(out(BF16, SEQ, D)...  24.2 us
    unnamed x25, local copies, waits for them, and re-layouts  12.7 us

profile of v1, /device:TPU:0, one launch (start us, length us, event | category | flops | bytes accessed | tf_op | source)
XLA Modules:
  0.0 310.2 jit_solution(2715542223752184374)
XLA Ops:
  0.6 0.9 constant_dynamic-update-slice_fusion.1
  1.5 0.9 constant_dynamic-update-slice_fusion
  2.4 0.9 fusion
  3.3 0.8 fusion.1
  4.1 0.7 bitcast_dynamic-update-slice_fusion
  4.9 0.8 copy.58
  5.9 0.8 copy.57
  6.7 0.7 copy.60
  7.4 0.7 copy.61
  8.3 0.7 copy-done
  9.0 54.8 %gather_all.1 = bf16[16,4,2,2,2,24,384]{6,5,4,3,2,1,0:T(8,128)(2,1)} custom-call(bf16[16,24,384]{2,1,0:T(8,128)(2,1)} %copy-done), custom_call_target="tpu_custom_call" | custom-call | tf_op jit(solution)/shard_map/gather_all/pallas_call | solution.py:190
  63.8 1.1 slice.61
  65.3 0.6 pad.27.depth_ref
  67.9 0.6 pad_bitcast_fusion.kmt_ref
  68.5 24.2 %mixer_forward.1 = (bf16[2,512,768]{2,1,0:T(8,128)(2,1)}, bf16[2,512,1536]{2,1,0:T(8,128)(2,1)}, bf16[2,512,768]{2,1,0:T(8,128)(2,1)}, f32[2,512,384]{2,1,0:T(8,...) custom-call(s32[2]{0:T(128)} %len_ref.5, bf16[2,512,768]{2,1,0:T(8,128)(2,1)} %hid_ref.1, ...), custom_call_target="tpu_custom_call" | custom-call | tf_op jit(solution)/shard_map/mixer_forward/pallas_call | solution.py:336
  93.3 77.5 %feed_forward.1 = (bf16[1024,768]{1,0:T(8,128)(2,1)}, bf16[4,1024,768]{2,1,0:T(8,128)(2,1)}, bf16[4,1024,768]{2,1,0:T(8,128)(2,1)}, bf16[2,1024,384]{2,1,0:T(8,1...) custom-call(s32[2]{0:T(128)} %len_ref.5, ...), custom_call_target="tpu_custom_call" | custom-call | tf_op jit(solution)/shard_map/feed_forward/pallas_call | solution.py:543
  170.9 38.2 %mixer_backward.1 = (bf16[4,1024,384]{2,1,0:T(8,128)(2,1)}, bf16[2,512,384]{2,1,0:T(8,128)(2,1)}, bf16[2,512,768]{2,1,0:T(8,128)(2,1)}, f32[72,384]{1,0:T(8,128)}, f32[9,8,768]{2,1,0:T(8,128)}) custom-call(s32[2]{0:T(128)} %len_ref.5, bf16[2,512,768]{2,1,0:T(8,128)(2,1)} %get-tuple-element.36.x_ref, bf16[2,512,1536]{2,1,0:T(8,128)(2,1)} %get-tuple-element.38.proj_ref, ...), custom_call_target="tpu_custom_call" | custom-call | tf_op jit(solution)/shard_map/mixer_backward/pallas_call | solution.py:740
  209.1 0.9 convert_bitcast_fusion
  212.0 0.9 pad.30.clone
  213.0 0.6 reduce_sum.39
  215.0 83.7 %scatter_all.1 = (f32[16,24,384]{2,1,0:T(8,128)}, f32[8,128]{1,0:T(8,128)}) custom-call(bf16[1024,768]{1,0:T(8,128)(2,1)} %bitcast.112, bf16[1024,768]{1,0:T(8,128)(2,1)} %bitcast.113, bf16[4,1024,384]{2,1,0:T(8,128)(2,1)} %get-tuple-element.46.gproj_ref, bf16[1024,384]{1,0:T(8,128)(2,1)} %bitcast.125, bf16[1024,768]{1,0:T(8,128)(2,1)} %bitcast.115, ...), custom_call_target="tpu_custom_call" | custom-call | tf_op jit(solution)/shard_map/scatter_all/pallas_call | solution.py:1197
  298.6 1.3 slice.79
  300.6 1.2 sqrt_bitcast_fusion
  301.8 1.8 fusion.13
  303.5 0.7 copy.83
  304.2 1.4 slice_bitcast_fusion.3
  305.9 0.7 copy.75
  306.6 0.9 slice_bitcast_fusion.1
  307.5 0.6 copy.84
  308.2 0.6 copy.76
  308.9 0.6 copy.77
  309.5 0.7 copy.74
  (42 shorter events, 6.3 us)
Async XLA Ops:
  8.3 0.7 copy-start
  210.0 1.6 copy-start.1
  210.6 1.1 copy-start.2
  211.0 2.0 copy-start.3

commit v2 on v1

--- a/solution.py
+++ b/solution.py
@@ -374,6 +374,7 @@
 
 TILE = 256
 CHUNK = 16
+PART = 256
 
 
 def ffn_kernel(
@@ -455,25 +456,40 @@
 
     lax.fori_loop(0, TILE // CHUNK, norm_one, 0)
 
-    for s in range(4):
+    def part_of(c):
+        return c // 3, pl.ds(c % 3 * PART, PART)
+
+    def expand(c):
+        s, units = part_of(c)
+        pre[c % 2] = nt(fb_ref[s // 2], wup_ref[s, units])
+
+    def gelu(c):
+        s, units = part_of(c)
+        for r in range(TILE // 32):
+            rows = slice(r * 32, (r + 1) * 32)
+            v = pre[c % 2, rows]
+            phi = 0.5 + 0.5 * lax.erf(v * math.sqrt(0.5))
+            act_ref[s, rows, units] = (v * phi).astype(BF16)
+            dg[s, rows, units] = phi + v * jnp.exp(v * v * -0.5) * (1.0 / math.sqrt(2.0 * math.pi))
+
+    def contract(s):
         g = s // 2
-        pre[...] = nt(fb_ref[g], wup_ref[s])
-
-        def gelu(i, carry):
-            rows = rows_of(i)
-            v = pre[rows]
-            phi = 0.5 + 0.5 * lax.erf(v * math.sqrt(0.5))
-            act_ref[s, rows] = (v * phi).astype(BF16)
-            dg[s, rows] = phi + v * jnp.exp(v * v * -0.5) * (1.0 / math.sqrt(2.0 * math.pi))
-            return carry
-
-        lax.fori_loop(0, TILE // CHUNK, gelu, 0)
         part = nn(act_ref[s], wdn_ref[s])
         lanes = slice(g * W, (g + 1) * W)
         if s % 2 == 0:
             ffn[:, lanes] = part
         else:
             ffn[:, lanes] += part
+
+    parts = 4 * D // PART
+    expand(0)
+    for c in range(parts):
+        if c + 1 < parts:
+            expand(c + 1)
+        if c % 3 == 0 and c > 0:
+            contract(c // 3 - 1)
+        gelu(c)
+    contract(3)
 
     def norm_two(i, carry):
         rows = rows_of(i)
@@ -495,18 +511,12 @@
 
     lax.fori_loop(0, TILE // CHUNK, norm_two, 0)
 
-    for s in range(4):
-        g = s // 2
-        lanes = slice(g * W, (g + 1) * W)
-        pre[...] = nt(gffn_ref[g], wdn_ref[s])
-
-        def times(i, carry):
-            rows = rows_of(i)
-            gpre_ref[s, rows] = (pre[rows] * dg[s, rows]).astype(BF16)
-            return carry
-
-        lax.fori_loop(0, TILE // CHUNK, times, 0)
-        gr2[:, lanes] += nn(gpre_ref[s], wup_ref[s])
+    for c in range(parts):
+        s, units = part_of(c)
+        gpre_ref[s, :, units] = (nt(gffn_ref[s // 2], wdn_ref[s, units]) * dg[s, :, units]).astype(BF16)
+        if c % 3 == 2:
+            lanes = slice(s // 2 * W, (s // 2 + 1) * W)
+            gr2[:, lanes] += nn(gpre_ref[s], wup_ref[s])
 
     def norm_one_back(i, carry):
         rows = rows_of(i)
@@ -581,7 +591,7 @@
             pltpu.VMEM((TILE, D), F32),
             pltpu.VMEM((TILE, 128), F32),
             pltpu.VMEM((TILE, D), F32),
-            pltpu.VMEM((TILE, D), F32),
+            pltpu.VMEM((2, TILE, PART), F32),
             pltpu.VMEM((4, TILE, D), F32),
             pltpu.VMEM((TILE, D), F32),
         ],
@@ -1105,6 +1115,28 @@
         def _():
             work(t)
 
+    def sums(t):
+        for k in range(3):
+
+            @pl.when(t == 3 * k + 3)
+            def _():
+                t_copy(k).wait_recv()
+                tiny[k + 1] = tiny[k] + got[k]
+                if k < 2:
+                    t_copy(k + 1).start()
+
+        @pl.when(t == 10)
+        def _():
+            for d in range(1, depth):
+
+                @pl.when(z + d < depth)
+                def _():
+                    t_line(d, 1).start()
+
+                @pl.when(z >= d)
+                def _():
+                    t_line(d, -1).start()
+
     def tick(t, carry):
         stage(t, multiply)
         stage(t - 1, stage_core)
@@ -1112,24 +1144,10 @@
         stage(t - 5, stage_second)
         stage(t - 5 - z, stage_up)
         stage(t - 5 - (depth - 1 - z), stage_down)
+        sums(t)
         return carry
 
     lax.fori_loop(0, BLOCKS + 5 + depth, tick, 0)
-
-    for k in range(3):
-        t_copy(k).wait_recv()
-        tiny[k + 1] = tiny[k] + got[k]
-        if k < 2:
-            t_copy(k + 1).start()
-    for d in range(1, depth):
-
-        @pl.when(z + d < depth)
-        def _():
-            t_line(d, 1).start()
-
-        @pl.when(z >= d)
-        def _():
-            t_line(d, -1).start()
 
     for level in range(depth):
 

time: 311 us -> 291 us (0.936)
  Pallas kernels: 278 us -> 258 us
    pallas_call x1, Pallas kernels: 77.5 us -> 64.3 us  [feed_forward(): pl.pallas_call(ffn_kernel, grid=(tokens // TILE,), out_shape=(out(BF16, D...]
    pallas_call x1, Pallas kernels: 83.7 us -> 76.5 us  [scatter_all(): pl.pallas_call(functools.partial(scatter_kernel, depth), out_shape=(jax.S...]
where the time goes in v2:
time: 291 us; the launch traced here: 290 us
  Pallas kernels  258 us (89%)
  local copies, waits for them, and re-layouts  26.4 us (9%)
  other arithmetic  3.25 us (1%)
    pallas_call x1, Pallas kernels, scatter_all(): pl.pallas_call(functools.partial(scatter_kernel, depth), out_shape=(jax.S...  76.5 us
    pallas_call x1, Pallas kernels, feed_forward(): pl.pallas_call(ffn_kernel, grid=(tokens // TILE,), out_shape=(out(BF16, D...  64.3 us
    pallas_call x1, Pallas kernels, gather_all(): pl.pallas_call(functools.partial(gather_kernel, depth), out_shape=jax.Sha...  54.8 us
    pallas_call x1, Pallas kernels, backward(): pl.pallas_call(backward_kernel, grid=(rows,), out_shape=(jax.ShapeDtypeSt...  38.2 us
    pallas_call x1, Pallas kernels, forward(): pl.pallas_call(forward_kernel, grid=(rows,), out_shape=(out(BF16, SEQ, D)...  24.2 us
    unnamed x25, local copies, waits for them, and re-layouts  12.8 us

profile of v2, /device:TPU:0, one launch (start us, length us, event | category | flops | bytes accessed | tf_op | source)
XLA Modules:
  0.0 289.7 jit_solution(10257094392800782743)
XLA Ops:
  0.6 0.9 constant_dynamic-update-slice_fusion.1
  1.5 0.9 constant_dynamic-update-slice_fusion
  2.4 0.9 fusion
  3.3 0.8 fusion.1
  4.1 0.7 bitcast_dynamic-update-slice_fusion
  4.9 0.8 copy.58
  5.9 0.8 copy.57
  6.7 0.7 copy.60
  7.4 0.7 copy.61
  8.3 0.7 copy-done
  9.0 54.8 %gather_all.1 = bf16[16,4,2,2,2,24,384]{6,5,4,3,2,1,0:T(8,128)(2,1)} custom-call(bf16[16,24,384]{2,1,0:T(8,128)(2,1)} %copy-done), custom_call_target="tpu_custom_call" | custom-call | tf_op jit(solution)/shard_map/gather_all/pallas_call | solution.py:190
  63.8 1.1 slice.61
  65.3 0.6 pad.27.depth_ref
  67.9 0.6 pad_bitcast_fusion.kmt_ref
  68.5 24.2 %mixer_forward.1 = (bf16[2,512,768]{2,1,0:T(8,128)(2,1)}, bf16[2,512,1536]{2,1,0:T(8,128)(2,1)}, bf16[2,512,768]{2,1,0:T(8,128)(2,1)}, f32[2,512,384]{2,1,0:T(8,...) custom-call(s32[2]{0:T(128)} %len_ref.5, bf16[2,512,768]{2,1,0:T(8,128)(2,1)} %hid_ref.1, ...), custom_call_target="tpu_custom_call" | custom-call | tf_op jit(solution)/shard_map/mixer_forward/pallas_call | solution.py:336
  93.3 64.3 %feed_forward.1 = (bf16[1024,768]{1,0:T(8,128)(2,1)}, bf16[4,1024,768]{2,1,0:T(8,128)(2,1)}, bf16[4,1024,768]{2,1,0:T(8,128)(2,1)}, bf16[2,1024,384]{2,1,0:T(8,1...) custom-call(s32[2]{0:T(128)} %len_ref.5, ...), custom_call_target="tpu_custom_call" | custom-call | tf_op jit(solution)/shard_map/feed_forward/pallas_call | solution.py:553
  157.6 38.2 %mixer_backward.1 = (bf16[4,1024,384]{2,1,0:T(8,128)(2,1)}, bf16[2,512,384]{2,1,0:T(8,128)(2,1)}, bf16[2,512,768]{2,1,0:T(8,128)(2,1)}, f32[72,384]{1,0:T(8,128)}, f32[9,8,768]{2,1,0:T(8,128)}) custom-call(s32[2]{0:T(128)} %len_ref.5, bf16[2,512,768]{2,1,0:T(8,128)(2,1)} %get-tuple-element.36.x_ref, bf16[2,512,1536]{2,1,0:T(8,128)(2,1)} %get-tuple-element.38.proj_ref, ...), custom_call_target="tpu_custom_call" | custom-call | tf_op jit(solution)/shard_map/mixer_backward/pallas_call | solution.py:750
  195.9 0.9 convert_bitcast_fusion
  198.7 0.9 pad.30.clone
  199.8 0.6 reduce_sum.39
  201.7 76.5 %scatter_all.1 = (f32[16,24,384]{2,1,0:T(8,128)}, f32[8,128]{1,0:T(8,128)}) custom-call(bf16[1024,768]{1,0:T(8,128)(2,1)} %bitcast.112, bf16[1024,768]{1,0:T(8,128)(2,1)} %bitcast.113, bf16[4,1024,384]{2,1,0:T(8,128)(2,1)} %get-tuple-element.46.gproj_ref, bf16[1024,384]{1,0:T(8,128)(2,1)} %bitcast.125, bf16[1024,768]{1,0:T(8,128)(2,1)} %bitcast.115, ...), custom_call_target="tpu_custom_call" | custom-call | tf_op jit(solution)/shard_map/scatter_all/pallas_call | solution.py:1215
  278.2 1.3 slice.79
  280.1 1.2 sqrt_bitcast_fusion
  281.3 1.8 fusion.13
  283.1 0.7 copy.83
  283.8 1.4 slice_bitcast_fusion.3
  285.5 0.7 copy.75
  286.2 0.9 slice_bitcast_fusion.1
  287.1 0.6 copy.84
  287.8 0.6 copy.76
  288.4 0.6 copy.77
  289.1 0.7 copy.74
  (42 shorter events, 6.3 us)
Async XLA Ops:
  8.3 0.7 copy-start
  196.8 1.6 copy-start.1
  197.3 1.1 copy-start.2
  197.8 2.0 copy-start.3

commit v3 on v2

--- a/solution.py
+++ b/solution.py
@@ -237,7 +237,8 @@
 def forward_kernel(
     len_ref,
     hid_ref,
-    win_ref,
+    wa_ref,
+    wb_ref,
     wpt_ref,
     depth_ref,
     kmt_ref,
@@ -263,7 +264,7 @@
     sv[PAD + SEQ :] = jnp.zeros((PAD, W), F32)
 
     for b in range(4):
-        part = nn(x_ref[0], win_ref[b]).astype(BF16)
+        part = nn(x_ref[0], (wa_ref, wb_ref)[b // 2][b % 2]).astype(BF16)
         proj_ref[0, :, b * W : (b + 1) * W] = part
         if b == 3:
             sv[PAD : PAD + SEQ] = part.astype(F32)
@@ -348,7 +349,8 @@
         in_specs=[
             pl.BlockSpec(memory_space=pltpu.SMEM),
             per_row(SEQ, D),
-            pl.BlockSpec((4, D, W), lambda r: (2, 0, 0)),
+            pl.BlockSpec((2, D, W), lambda r: (5, 0, 0)),
+            pl.BlockSpec((2, D, W), lambda r: (6, 0, 0)),
             pl.BlockSpec((1, D, W), lambda r: (14, 0, 0)),
             pl.BlockSpec((16, D), lambda r: (0, 0)),
             pl.BlockSpec((8 * K, W), lambda r: (0, 0)),
@@ -369,7 +371,7 @@
         ],
         compiler_params=pltpu.CompilerParams(vmem_limit_bytes=56 * 1024 * 1024),
         name="mixer_forward",
-    )(lengths, hidden, full, full, depth, kmt)
+    )(lengths, hidden, full, full, full, depth, kmt)
 
 
 TILE = 256
@@ -569,7 +571,7 @@
             per_tile(D),
             per_tile(D),
             per_tile(D),
-            pl.BlockSpec((2, D, W), lambda i: (6, 0, 0)),
+            pl.BlockSpec((2, D, W), lambda i: (4, 0, 0)),
             pl.BlockSpec((4, D, W), lambda i: (0, 0, 0)),
             pl.BlockSpec((4, D, W), lambda i: (1, 0, 0)),
             pl.BlockSpec((8, D), lambda i: (0, 0)),
@@ -610,7 +612,8 @@
     lse_ref,
     gctx_ref,
     gr1_ref,
-    win_ref,
+    wa_ref,
+    wb_ref,
     wpt_ref,
     depth_ref,
     kmt_ref,
@@ -734,7 +737,7 @@
     lax.fori_loop(0, HEADS // 2, pair, 0)
 
     for b in range(4):
-        gs[...] += nt(gproj_ref[b], win_ref[b])
+        gs[...] += nt(gproj_ref[b], (wa_ref, wb_ref)[b // 2][b % 2])
     gin_ref[0] = jnp.where(inside, gr1_ref[0] + gs[...], 0.0).astype(BF16)
 
 
@@ -767,7 +770,8 @@
             per_row(8, SEQ),
             per_row(SEQ, D),
             per_row(SEQ, D),
-            pl.BlockSpec((4, D, W), lambda r: (2, 0, 0)),
+            pl.BlockSpec((2, D, W), lambda r: (5, 0, 0)),
+            pl.BlockSpec((2, D, W), lambda r: (6, 0, 0)),
             pl.BlockSpec((1, D, W), lambda r: (14, 0, 0)),
             pl.BlockSpec((16, D), lambda r: (0, 0)),
             pl.BlockSpec((8 * K, W), lambda r: (0, 0)),
@@ -791,7 +795,7 @@
         ],
         compiler_params=pltpu.CompilerParams(vmem_limit_bytes=56 * 1024 * 1024),
         name="mixer_backward",
-    )(lengths, x, proj, dl, kc, wt, lse, gctx, gr1, full, full, depth, kmt)
+    )(lengths, x, proj, dl, kc, wt, lse, gctx, gr1, full, full, full, depth, kmt)
 
 
 def pack(in_weight, depth_kernel, point_weight, kernel_weight, out_weight, up_weight, down_weight, norm_gains, norm_biases):
@@ -807,8 +811,8 @@
         [
             halves(down_weight),
             halves(up_weight.transpose(0, 2, 1)),
+            out_weight.reshape(rows, 2, W).transpose(1, 0, 2),
             in_weight.reshape(rows, 4, W).transpose(1, 0, 2),
-            out_weight.reshape(rows, 2, W).transpose(1, 0, 2),
             point_weight[None],
             small[None],
         ],
@@ -821,11 +825,11 @@
     small = shard[15]
     kernel = small[:, K : 4 * K].reshape(rows, K, 3).transpose(1, 0, 2).reshape(K, 3 * rows)
     return (
-        shard[8:12].transpose(1, 0, 2).reshape(rows, 4 * W),
+        shard[10:14].transpose(1, 0, 2).reshape(rows, 4 * W),
         small[:, :K].T,
         shard[14],
         kernel,
-        shard[12:14].transpose(1, 0, 2).reshape(rows, 2 * W),
+        shard[8:10].transpose(1, 0, 2).reshape(rows, 2 * W),
         shard[4:8].reshape(G, 2 * rows, W).transpose(0, 2, 1),
         shard[0:4].reshape(G, 2 * rows, W),
         small[:, 4 * K : 4 * K + 2].T,
@@ -833,38 +837,37 @@
     )
 
 
-def layer(hidden, lengths, full, out_grad):
-    rows = hidden.shape[0]
-    tokens = rows * SEQ
+def constants(full):
     small = full[15].astype(F32)
     depth = jnp.pad(small[:, :K].T, ((0, 16 - K), (0, 0)))
     kernel = small[:, K : 4 * K].reshape(D, K, 3).transpose(1, 0, 2).reshape(K, W, HEADS)
     kmt = jnp.pad(kernel.transpose(0, 2, 1), ((0, 0), (0, 8 - HEADS), (0, 0)))
     kmt = kmt.reshape(8 * K, W).astype(BF16)
     gb = jnp.pad(small[:, 4 * K : 4 * K + 4].T, ((0, 4), (0, 0)))
-
+    return depth, kmt, gb
+
+
+def layer(mesh, hidden, lengths, full, out_grad):
+    rows = hidden.shape[0]
+    tokens = rows * SEQ
+    depth, kmt, gb = constants(full)
     x, proj, dl, kc, wt, lse, ctx = forward(lengths, hidden, full, depth, kmt)
     flat_x, flat_ctx = x.reshape(tokens, D), ctx.reshape(tokens, D)
     y, act, gpre, fb, gffn, gmix, gr1, gctx, stat = feed_forward(
         lengths, flat_ctx, flat_x, out_grad.reshape(tokens, D), full, gb
     )
+    gctx, gr1 = gctx.reshape(rows, SEQ, D), gr1.reshape(rows, SEQ, D)
+    if fused(mesh, rows):
+        gin, shard, totals = backward_scatter(
+            mesh, lengths, x, proj, dl, kc, wt, lse, gctx, gr1, full, depth, kmt, ctx, gmix, act, gffn, gpre, fb, stat
+        )
+        return y.reshape(rows, SEQ, D), gin, shard, totals
     gproj, gkc, gin, gkm, gdk = backward(
-        lengths,
-        x,
-        proj,
-        dl,
-        kc,
-        wt,
-        lse,
-        gctx.reshape(rows, SEQ, D),
-        gr1.reshape(rows, SEQ, D),
-        full,
-        depth,
-        kmt,
+        lengths, x, proj, dl, kc, wt, lse, gctx, gr1, full, depth, kmt
     )
     stat = jnp.sum(stat, axis=1)
     grad_kernel = gkm.reshape(K, 8, W)[:, :HEADS].transpose(0, 2, 1).reshape(K, D, 3)
-    grad_small = jnp.concatenate(
+    small = jnp.concatenate(
         [
             jnp.sum(gdk, axis=1).T,
             grad_kernel.transpose(1, 0, 2).reshape(D, 3 * K),
@@ -872,51 +875,88 @@
         ],
         axis=1,
     )
-    grad_small = jnp.pad(grad_small, ((0, 0), (0, W - grad_small.shape[1]))).astype(BF16)
-    factors = (
-        flat_x,
-        dl.reshape(tokens, D),
-        gproj,
-        gkc.reshape(tokens, W),
-        flat_ctx,
-        gmix,
-        act,
-        gffn,
-        gpre,
-        fb,
+    small = jnp.pad(small, ((0, 0), (0, W - small.shape[1]))).astype(BF16)
+    local = weight_grads(
+        flat_x, dl.reshape(tokens, D), gproj, gkc.reshape(tokens, W), flat_ctx, gmix, act, gffn, gpre, fb, small
     )
-    sums = jnp.sum(stat[0:4], axis=1)
-    count = jnp.sum(lengths).astype(F32)
-    tiny = jnp.pad(jnp.concatenate([sums, count[None]]), (0, 123))
-    tiny = jnp.broadcast_to(tiny[None], (8, 128))
-    return y.reshape(rows, SEQ, D), gin, factors, grad_small, tiny
+    sums = jnp.concatenate([jnp.sum(stat[0:4], axis=1), jnp.sum(lengths).astype(F32)[None]])
+    if mesh is None:
+        return y.reshape(rows, SEQ, D), gin, local.astype(F32), sums[None]
+    devices = mesh.shape["dp"] * mesh.shape["fsdp"]
+    shard = lax.psum_scatter(
+        local.reshape(BLOCKS, devices, D // devices, W),
+        ("dp", "fsdp"),
+        scatter_dimension=1,
+        tiled=False,
+    )
+    return (
+        y.reshape(rows, SEQ, D),
+        gin,
+        shard.astype(F32),
+        lax.psum(sums, ("dp", "fsdp"))[None],
+    )
+
+
+def fused(mesh, rows):
+    return mesh is not None and mesh.shape["fsdp"] == 2 and mesh.shape["dp"] % 4 == 0 and rows == 2
 
 
 def weight_grads(x, dl, gproj, gkc, ctx, gmix, act, gffn, gpre, fb, small):
     pairs = [(act[s], gffn[s // 2]) for s in range(4)]
     pairs += [(gpre[s], fb[s // 2]) for s in range(4)]
+    pairs += [(ctx, gmix[b]) for b in range(2)]
     pairs += [(x, gproj[b]) for b in range(4)]
-    pairs += [(ctx, gmix[b]) for b in range(2)]
     pairs += [(dl, gkc)]
     return jnp.stack([tn(a, b).astype(BF16) for a, b in pairs] + [small])
 
 
-def scatter_kernel(
+def backward_scatter_kernel(
     depth,
+    len_ref,
+    x_hbm,
+    proj_hbm,
+    dl_hbm,
+    kc_hbm,
+    wt_hbm,
+    lse_hbm,
+    gctx_hbm,
+    gr1_hbm,
+    full_hbm,
+    depth_ref,
+    kmt_ref,
+    ctx_hbm,
+    gmix_hbm,
+    act_hbm,
+    gffn_hbm,
+    gpre_hbm,
+    fb_hbm,
+    stat_ref,
+    gin_ref,
+    o_ref,
+    u_ref,
     x_ref,
+    proj_ref,
     dl_ref,
+    kc_ref,
+    wt_ref,
+    lse_ref,
+    gctx_ref,
+    gr1_ref,
+    win_ref,
+    wpt_ref,
     gproj_ref,
     gkc_ref,
-    ctx_ref,
-    gmix_ref,
-    act_ref,
-    gffn_ref,
-    gpre_ref,
-    fb_ref,
-    small_ref,
-    t_ref,
-    o_ref,
-    u_ref,
+    gkm,
+    gdk,
+    small,
+    sv,
+    gc,
+    xs,
+    gd,
+    gs,
+    gq,
+    gt,
+    dqt,
     left,
     right,
     part,
@@ -927,6 +967,7 @@
     rd,
     tiny,
     got,
+    in_sem,
     left_sem,
     right_sem,
     cs,
@@ -946,6 +987,8 @@
     c_dev, x_dev, y_dev = partners(dp, x, core, y)
     up_dev, down_dev = (dp + 4, y), (dp - 4, y)
     last = BLOCKS - 1
+    rows = x_ref.shape[0]
+    early = 5 * rows
 
     def fetch(t, act):
         def both(a, b):
@@ -958,23 +1001,23 @@
 
         @pl.when(t < 4)
         def _():
-            both(act_ref.at[t], gffn_ref.at[t // 2])
+            both(act_hbm.at[t], gffn_hbm.at[t // 2])
 
         @pl.when((t >= 4) & (t < 8))
         def _():
-            both(gpre_ref.at[t - 4], fb_ref.at[(t - 4) // 2])
-
-        @pl.when((t >= 8) & (t < 12))
-        def _():
-            both(x_ref, gproj_ref.at[t - 8])
-
-        @pl.when((t >= 12) & (t < 14))
-        def _():
-            both(ctx_ref, gmix_ref.at[t - 12])
+            both(gpre_hbm.at[t - 4], fb_hbm.at[(t - 4) // 2])
+
+        @pl.when((t >= 8) & (t < 10))
+        def _():
+            both(ctx_hbm, gmix_hbm.at[t - 8])
+
+        @pl.when((t >= 10) & (t < 14))
+        def _():
+            both(x_hbm, gproj_ref.at[:, t - 10])
 
         @pl.when(t == 14)
         def _():
-            both(dl_ref, gkc_ref)
+            both(dl_hbm, gkc_ref)
 
     def c_copy(t):
         return send(part.at[t, :, :, 1 - core], rc.at[t], cs.at[t], cr.at[t], c_dev)
@@ -1024,16 +1067,189 @@
         def _():
             work(False)
 
+
+    def inside_of(r):
+        return lax.broadcasted_iota(jnp.int32, (SEQ, 1), 0) < len_ref[r]
+
+    def piece_span(r):
+        sv[PAD : PAD + SEQ] = proj_ref[r, :, 3 * W :].astype(F32)
+        gc[PAD : PAD + SEQ] = gctx_ref[r, :, W:].astype(F32)
+        xs[PAD : PAD + SEQ] = x_ref[r].astype(F32)
+
+        e16 = spread(16)
+        place_row = lax.broadcasted_iota(jnp.int32, (W, 128), 0) // HD
+        place_col = lax.broadcasted_iota(jnp.int32, (W, 128), 1)
+        both = []
+        for k in range(K):
+            weight = pltpu.roll(wt_ref[r, k * 8 : k * 8 + 8], (k - K // 2) % SEQ, 1)
+            high = weight.astype(BF16).astype(F32)
+            both.append(jnp.concatenate([high, weight - high], axis=0).astype(BF16))
+        for n in range(4):
+            rows = slice(n * 128, (n + 1) * 128)
+            spans = jnp.zeros((128, 128), F32)
+            total = jnp.zeros((128, W), F32)
+            for k in range(K):
+                start = PAD + n * 128 + k - K // 2
+                product_k = gc[PAD + n * 128 : PAD + (n + 1) * 128] * sv[start : start + 128]
+                chosen = (place_col == place_row + 8 * k).astype(F32).astype(BF16)
+                spans = spans + nn(product_k.astype(BF16), chosen)
+                start = PAD + n * 128 - k + K // 2
+                total = total + tn(both[k][:, rows], e16) * gc[start : start + 128]
+            gt[:, rows] = spans.T
+            gproj_ref[r, 3, rows] = total.astype(BF16)
+
+    def piece_logits(r):
+        center = jnp.zeros((8, SEQ), F32)
+        for k in range(K):
+            center = center + wt_ref[r, k * 8 : k * 8 + 8] * gt[k * 8 : k * 8 + 8]
+        glt = jnp.concatenate(
+            [
+                wt_ref[r, k * 8 : k * 8 + 8] * (gt[k * 8 : k * 8 + 8] - center)
+                for k in range(K)
+            ],
+            axis=0,
+        ).astype(BF16)
+        query = proj_ref[r, :, 0:W].astype(F32)
+        mk = (kc_ref[r] * query).astype(BF16)
+        gkm[...] += nn(glt, mk)
+        mixed = tn(glt, kmt_ref[...])
+        gkc_ref[r] = (mixed * query).astype(BF16)
+        gq[...] = mixed * kc_ref[r]
+        gd[PAD : PAD + SEQ] = nt(gkc_ref[r], wpt_ref[0])
+
+
+    def piece_columns(r):
+        def column(c, carry):
+            lane = pl.ds(pl.multiple_of(c * 128, 128), 128)
+            sums = [jnp.zeros((8, 128), F32)] * K
+            for n in range(8):
+                total = jnp.zeros((64, 128), F32)
+                center = PAD + n * 64
+                grad = gd[center : center + 64, lane]
+                for k in range(K):
+                    start = center + k - K // 2
+                    sums[k] = sums[k] + jnp.sum(
+                        (xs[start : start + 64, lane] * grad).reshape(8, 8, 128), axis=0
+                    )
+                    start = center - k + K // 2
+                    total = total + gd[start : start + 64, lane] * depth_ref[k : k + 1, lane]
+                gs[n * 64 : (n + 1) * 64, lane] = total
+            for k in range(K):
+                gdk[k, :, lane] = gdk[k, :, lane] + sums[k]
+            return carry
+
+        lax.fori_loop(0, D // 128, column, 0)
+
+
+    def piece_pairs(r, first, stop):
+        inside = inside_of(r)
+        lane_head = lax.broadcasted_iota(jnp.int32, (1, 128), 1) // HD
+        bias = jnp.where(inside, 0.0, -1e30).astype(F32)
+
+        def pair(p, carry):
+            def lanes(part):
+                return pl.ds(pl.multiple_of(part * W + p * 128, 128), 128)
+
+            q2, k2, v2 = (proj_ref[r, :, lanes(part)] for part in range(3))
+            g2 = gctx_ref[r, :, lanes(0)]
+            results = []
+            for h in range(2):
+                mine = lane_head == h
+                scale = jnp.where(mine, 1.0 / math.sqrt(HD), 0.0).astype(BF16)
+                scores = nt(k2, q2 * scale) + bias
+                probs = jnp.exp(scores - lse_ref[r, pl.ds(p * 2 + h, 1)])
+                grads = nt(v2 * jnp.where(mine, 1.0, 0.0).astype(BF16), g2)
+                correction = jnp.sum(probs * grads, axis=0, keepdims=True)
+                grad_scores = (probs * (grads - correction)).astype(BF16)
+                dqt[h * HD : (h + 1) * HD] = tn(k2, grad_scores)[h * HD : (h + 1) * HD]
+                results.append((nn(grad_scores, q2), nn(probs.astype(BF16), g2)))
+            low = lane_head == 0
+            scale = 1.0 / math.sqrt(HD)
+            gproj_ref[r, 0, :, lanes(0)] = (dqt[...].T * scale + gq[:, lanes(0)]).astype(BF16)
+            gproj_ref[r, 1, :, lanes(0)] = (jnp.where(low, results[0][0], results[1][0]) * scale).astype(BF16)
+            gproj_ref[r, 2, :, lanes(0)] = jnp.where(low, results[0][1], results[1][1]).astype(BF16)
+            return carry
+
+        lax.fori_loop(first, stop, pair, 0)
+
+
+    def piece_inputs(r):
+        inside = inside_of(r)
+        for b in range(4):
+            gs[...] += nt(gproj_ref[r, b], win_ref[b])
+        gin_ref[r] = jnp.where(inside, gr1_ref[r] + gs[...], 0.0).astype(BF16)
+
+
+    def chosen(height, rule):
+        row = lax.broadcasted_iota(jnp.int32, (height, 128), 0)
+        lane = lax.broadcasted_iota(jnp.int32, (height, 128), 1)
+        return rule(row, lane).astype(F32).astype(BF16)
+
+    def gather_small():
+        taps = jnp.concatenate(
+            [jnp.sum(gdk[...], axis=1), jnp.zeros((16 - K, D), F32), jnp.sum(stat_ref[...], axis=1)]
+        ).astype(BF16)
+        pick = chosen(
+            24,
+            lambda row, lane: ((row < K) & (lane == row)) | ((row >= 20) & (lane == row - 20 + 4 * K)),
+        )
+        both = tn(taps, pick)
+        low = gkm[...].astype(BF16)
+        small[...] = both
+        for odd in range(2):
+            pick = chosen(
+                8 * K,
+                lambda row, lane: (row % 8 >= 3 * odd)
+                & (row % 8 < 3 * odd + 3)
+                & (lane == K + row // 8 * 3 + row % 8 - 3 * odd),
+            )
+            half = pl.ds(odd, W, stride=2)
+            small[half] = small[half] + tn(low, pick)
+
+    loads = (
+        (x_hbm, x_ref),
+        (proj_hbm, proj_ref),
+        (dl_hbm, dl_ref),
+        (kc_hbm, kc_ref),
+        (wt_hbm, wt_ref),
+        (lse_hbm, lse_ref),
+        (gctx_hbm, gctx_ref),
+        (gr1_hbm, gr1_ref),
+        (full_hbm.at[pl.ds(10, 4)], win_ref),
+        (full_hbm.at[pl.ds(14, 1)], wpt_ref),
+    )
+    inputs = [
+        pltpu.make_async_copy(source, target, in_sem.at[i])
+        for i, (source, target) in enumerate(loads)
+    ]
     fetch(0, lambda copy: copy.start())
+    for copy in inputs:
+        copy.start()
+    gkm[...] = jnp.zeros_like(gkm)
+    gdk[...] = jnp.zeros_like(gdk)
+    for ref, width in ((sv, W), (gc, W), (xs, D), (gd, D)):
+        ref[0:PAD] = jnp.zeros((PAD, width), F32)
+        ref[PAD + SEQ :] = jnp.zeros((PAD, width), F32)
     lines = tuple((z >= d, (dp - 4 * d, y)) for d in range(1, depth)) + tuple(
         (z + d < depth, (dp + 4 * d, y)) for d in range(1, depth)
     )
     meet((c_dev, x_dev, y_dev), lines)
-    tiny[0] = t_ref[...]
+    lane = lax.broadcasted_iota(jnp.int32, (8, 128), 1)
+    mine = jnp.zeros((8, 128), F32)
+    for k in range(4):
+        mine = jnp.where(lane == k, jnp.sum(stat_ref[k]), mine)
+    count = len_ref[0]
+    for r in range(1, rows):
+        count = count + len_ref[r]
+    tiny[0] = jnp.where(lane == 4, count.astype(F32), mine)
     t_copy(0).start()
 
     def multiply(t):
-        @pl.when(t + 1 < last)
+        @pl.when(t == early)
+        def _():
+            fetch(t, lambda copy: copy.start())
+
+        @pl.when((t + 1 < last) & (t + 1 != early))
         def _():
             fetch(t + 1, lambda copy: copy.start())
 
@@ -1042,7 +1258,8 @@
             fetch(t, lambda copy: copy.wait())
             slot = t % 2
             for c in range(2):
-                block = tn(left[slot, :, c * W : (c + 1) * W], right[slot])
+                a = left[slot, :, :, c * W : (c + 1) * W].reshape(rows * SEQ, W)
+                block = tn(a, right[slot].reshape(rows * SEQ, W))
                 half = depth // 2
                 part[t, c * half : (c + 1) * half] = block.reshape(
                     (half,) + part.shape[2:]
@@ -1050,7 +1267,9 @@
 
         @pl.when(t == last)
         def _():
-            part[t] = small_ref[...]
+            gather_small()
+            filled = jnp.concatenate([small[...], jnp.zeros((D, W - 128), F32)], axis=1)
+            part[t] = filled.reshape(part.shape[1:]).astype(BF16)
 
         c_copy(t).start()
 
@@ -1145,6 +1364,28 @@
         stage(t - 5 - z, stage_up)
         stage(t - 5 - (depth - 1 - z), stage_down)
         sums(t)
+        row = t // 5
+
+        def when(i, work):
+            @pl.when((t < early) & (t % 5 == i))
+            def _():
+                work()
+
+        @pl.when(t == 0)
+        def _():
+            for copy in inputs:
+                copy.wait()
+
+        when(0, lambda: piece_span(row))
+        when(1, lambda: piece_logits(row))
+        when(2, lambda: piece_columns(row))
+        when(3, lambda: piece_pairs(row, 0, 2))
+
+        def close():
+            piece_pairs(row, 2, 3)
+            piece_inputs(row)
+
+        when(4, close)
         return carry
 
     lax.fori_loop(0, BLOCKS + 5 + depth, tick, 0)
@@ -1195,52 +1436,96 @@
     lax.fori_loop(0, BLOCKS, finish, 0)
 
 
-def scatter_all(factors, small, tiny, mesh):
+def backward_scatter(mesh, lengths, x, proj, dl, kc, wt, lse, gctx, gr1, full, depth_kernel, kmt, ctx, gmix, act, gffn, gpre, fb, stat):
     dp, fsdp = mesh.shape["dp"], mesh.shape["fsdp"]
-    rows = D // (dp * fsdp)
-    if fsdp != 2 or dp % 4:
-        local = weight_grads(*factors, small)
-        shard = lax.psum_scatter(
-            local.reshape(BLOCKS, dp * fsdp, rows, W),
-            ("dp", "fsdp"),
-            scatter_dimension=1,
-            tiled=False,
-        )
-        return shard.astype(F32), lax.psum(tiny, ("dp", "fsdp"))
+    share = D // (dp * fsdp)
     depth = dp // 4
-    tokens = factors[0].shape[0]
+    rows = x.shape[0]
     dma = pltpu.SemaphoreType.DMA
     anywhere = pl.BlockSpec(memory_space=pl.ANY)
     inside = pl.BlockSpec(memory_space=pltpu.VMEM)
+
+    def by_row(values):
+        return values.reshape(values.shape[:-2] + (rows, SEQ, values.shape[-1]))
+
     return pl.pallas_call(
-        functools.partial(scatter_kernel, depth),
+        functools.partial(backward_scatter_kernel, depth),
         out_shape=(
-            jax.ShapeDtypeStruct((BLOCKS, rows, W), F32),
+            jax.ShapeDtypeStruct((rows, SEQ, D), BF16),
+            jax.ShapeDtypeStruct((BLOCKS, share, W), F32),
             jax.ShapeDtypeStruct((8, 128), F32),
         ),
-        in_specs=[anywhere] * len(factors) + [inside, inside],
-        out_specs=(inside, inside),
+        in_specs=[pl.BlockSpec(memory_space=pltpu.SMEM)]
+        + [anywhere] * 9
+        + [inside] * 2
+        + [anywhere] * 6
+        + [inside],
+        out_specs=(inside, inside, inside),
         scratch_shapes=[
-            pltpu.VMEM((2, tokens, D), BF16),
-            pltpu.VMEM((2, tokens, W), BF16),
-            pltpu.VMEM((BLOCKS, depth, 2, 2, 2, rows, W), BF16),
-            pltpu.VMEM((BLOCKS, depth, 2, 2, rows, W), BF16),
-            pltpu.VMEM((BLOCKS, depth, 2, rows, W), BF16),
-            pltpu.VMEM((BLOCKS, depth, rows, W), BF16),
-            pltpu.VMEM((BLOCKS, depth, rows, W), BF16),
-            pltpu.VMEM((BLOCKS, depth, rows, W), BF16),
+            pltpu.VMEM((rows, SEQ, D), BF16),
+            pltpu.VMEM((rows, SEQ, 4 * W), BF16),
+            pltpu.VMEM((rows, SEQ, D), BF16),
+            pltpu.VMEM((rows, SEQ, W), F32),
+            pltpu.VMEM((rows, 8 * K, SEQ), F32),
+            pltpu.VMEM((rows, 8, SEQ), F32),
+            pltpu.VMEM((rows, SEQ, D), BF16),
+            pltpu.VMEM((rows, SEQ, D), F32),
+            pltpu.VMEM((4, D, W), BF16),
+            pltpu.VMEM((1, D, W), BF16),
+            pltpu.VMEM((rows, 4, SEQ, W), BF16),
+            pltpu.VMEM((rows, SEQ, W), BF16),
+            pltpu.VMEM((8 * K, W), F32),
+            pltpu.VMEM((K, 8, D), F32),
+            pltpu.VMEM((D, 128), F32),
+            pltpu.VMEM((SEQ + 2 * PAD, W), F32),
+            pltpu.VMEM((SEQ + 2 * PAD, W), F32),
+            pltpu.VMEM((SEQ + 2 * PAD, D), F32),
+            pltpu.VMEM((SEQ + 2 * PAD, D), F32),
+            pltpu.VMEM((SEQ, D), F32),
+            pltpu.VMEM((SEQ, W), F32),
+            pltpu.VMEM((128, SEQ), F32),
+            pltpu.VMEM((128, SEQ), F32),
+            pltpu.VMEM((2, rows, SEQ, D), BF16),
+            pltpu.VMEM((2, rows, SEQ, W), BF16),
+            pltpu.VMEM((BLOCKS, depth, 2, 2, 2, share, W), BF16),
+            pltpu.VMEM((BLOCKS, depth, 2, 2, share, W), BF16),
+            pltpu.VMEM((BLOCKS, depth, 2, share, W), BF16),
+            pltpu.VMEM((BLOCKS, depth, share, W), BF16),
+            pltpu.VMEM((BLOCKS, depth, share, W), BF16),
+            pltpu.VMEM((BLOCKS, depth, share, W), BF16),
             pltpu.VMEM((4, 8, 128), F32),
             pltpu.VMEM((3 + depth, 8, 128), F32),
+            dma((10,)),
             dma((2,)),
             dma((2,)),
         ]
         + [dma((BLOCKS,))] * 10
         + [dma((1 + 2 * depth,)), dma((3 + depth,))],
         compiler_params=pltpu.CompilerParams(
-            collective_id=1, has_side_effects=True, vmem_limit_bytes=60 * 1024 * 1024
+            collective_id=1, has_side_effects=True, vmem_limit_bytes=67_000_000
         ),
-        name="scatter_all",
-    )(*factors, small.reshape(depth, 2, 2, 2, rows, W), tiny)
+        name="backward_scatter",
+    )(
+        lengths,
+        x,
+        proj,
+        dl,
+        kc,
+        wt,
+        lse,
+        gctx,
+        gr1,
+        full,
+        depth_kernel,
+        kmt,
+        ctx,
+        by_row(gmix),
+        by_row(act),
+        by_row(gffn),
+        by_row(gpre),
+        by_row(fb),
+        stat,
+    )
 
 
 def body(
@@ -1272,8 +1557,7 @@
         ),
         mesh,
     )
-    output, input_grad, factors, small, tiny = layer(hidden, lengths, full, out_grad)
-    shard, totals = scatter_all(factors, small, tiny, mesh)
+    output, input_grad, shard, totals = layer(mesh, hidden, lengths, full, out_grad)
     rms = jnp.sqrt(totals[0, :4] / (totals[0, 4] * D))
     return (output, input_grad) + unpack(shard) + (rms,)
 

time: 291 us -> 275 us (0.945)
  Pallas kernels: 258 us -> 247 us
    pallas_call x2 -> x1, Pallas kernels: 115 us -> 104 us  [backward_scatter(): pl.pallas_call(functools.partial(backward_scatter_kernel, depth), out_sha...]
    unnamed x25 -> x20, local copies, waits for them, and re-layouts: 12.8 us -> 13.2 us
where the time goes in v3:
time: 275 us; the launch traced here: 274 us
  Pallas kernels  247 us (90%)
  local copies, waits for them, and re-layouts  24.4 us (9%)
    pallas_call x1, Pallas kernels, backward_scatter(): pl.pallas_call(functools.partial(backward_scatter_kernel, depth), out_sha...  104 us
    pallas_call x1, Pallas kernels, feed_forward(): pl.pallas_call(ffn_kernel, grid=(tokens // TILE,), out_shape=(out(BF16, D...  64.3 us
    pallas_call x1, Pallas kernels, gather_all(): pl.pallas_call(functools.partial(gather_kernel, depth), out_shape=jax.Sha...  54.8 us
    pallas_call x1, Pallas kernels, forward(): pl.pallas_call(forward_kernel, grid=(rows,), out_shape=(out(BF16, SEQ, D)...  24.1 us
    unnamed x20, local copies, waits for them, and re-layouts  13.2 us

profile of v3, /device:TPU:0, one launch (start us, length us, event | category | flops | bytes accessed | tf_op | source)
XLA Modules:
  0.0 273.8 jit_solution(15159030840543105705)
XLA Ops:
  0.6 0.8 copy.54
  1.4 0.7 copy.57
  2.2 0.7 copy.58
  2.9 0.8 copy.55
  4.0 0.9 constant_dynamic-update-slice_fusion.1
  4.9 0.9 constant_dynamic-update-slice_fusion
  5.8 0.8 fusion.1
  6.5 0.9 fusion
  7.4 0.7 bitcast_dynamic-update-slice_fusion
  8.3 0.7 copy-done.1
  9.0 54.8 %gather_all.1 = bf16[16,4,2,2,2,24,384]{6,5,4,3,2,1,0:T(8,128)(2,1)} custom-call(bf16[16,24,384]{2,1,0:T(8,128)(2,1)} %copy-done.1), custom_call_target="tpu_custom_call" | custom-call | tf_op jit(solution)/shard_map/gather_all/pallas_call | solution.py:190
  63.8 1.1 slice.50
  65.6 0.6 pad.18.depth_ref
  66.2 0.6 pad.20.gb_ref
  66.8 0.6 copy.62
  67.4 0.5 reshape.123
  68.5 0.6 pad_bitcast_fusion.kmt_ref
  69.1 24.1 %mixer_forward.1 = (bf16[2,512,768]{2,1,0:T(8,128)(2,1)}, bf16[2,512,1536]{2,1,0:T(8,128)(2,1)}, bf16[2,512,768]{2,1,0:T(8,128)(2,1)}, f32[2,512,384]{2,1,0:T(8,...) custom-call(s32[2]{0:T(128)} %len_ref.5, bf16[2,512,768]{2,1,0:T(8,128)(2,1)} %hid_ref.1, ...), custom_call_target="tpu_custom_call" | custom-call | tf_op jit(solution)/shard_map/mixer_forward/pallas_call | solution.py:337
  93.2 64.3 %feed_forward.1 = (bf16[1024,768]{1,0:T(8,128)(2,1)}, bf16[4,1024,768]{2,1,0:T(8,128)(2,1)}, bf16[4,1024,768]{2,1,0:T(8,128)(2,1)}, bf16[2,1024,384]{2,1,0:T(8,1...) custom-call(s32[2]{0:T(128)} %len_ref.5, ...), custom_call_target="tpu_custom_call" | custom-call | tf_op jit(solution)/shard_map/feed_forward/pallas_call | solution.py:555
  157.5 103.5 %backward_scatter.1 = (bf16[2,512,768]{2,1,0:T(8,128)(2,1)}, f32[16,24,384]{2,1,0:T(8,128)}, f32[8,128]{1,0:T(8,128)}) custom-call(s32[2]{0:T(128)} %len_ref.5, bf16[2,512,768]{2,1,0:T(8,128)(2,1)} %get-tuple-element.32.x_hbm, bf16[2,512,1536]{2,1,0:T(8,128)(2,1)} %get-tuple-element.34.proj_hbm, bf16[2,512,768]{2,1,0:T(8,128)(2,1)} %get-tuple-element.35.dl_hbm, ...), custom_call_target="tpu_custom_call" | custom-call | tf_op jit(solution)/shard_map/backward_scatter/pallas_call | solution.py:1451
  261.1 1.4 slice.65
  263.1 1.2 sqrt_bitcast_fusion
  264.3 0.9 slice_bitcast_fusion.1
  265.2 0.6 copy.76
  265.8 1.4 slice_bitcast_fusion.3
  267.2 1.8 fusion.11
  269.3 0.7 copy.68
  269.9 0.6 copy.71
  270.6 0.6 copy.70
  271.4 0.7 copy.69
  272.0 0.7 copy.75
  272.7 1.1 copy.85
  (23 shorter events, 1.9 us)
Async XLA Ops:
  8.3 0.7 copy-start.1
  261.1 11.7 %copy-start = (bf16[2,512,768]{2,1,0:T(8,128)(2,1)S(1)}, bf16[2,512,768]{2,1,0:T(8,128)(2,1)}, u32[]{:S(2)}) copy-start(bf16[2,512,768]{2,1,0:T(8,128)(2,1)} %get-tuple-element.106) | copy-start | bytes 4718596

commit v4 on v3

--- a/solution.py
+++ b/solution.py
@@ -57,158 +57,11 @@
     )
 
 
-def gather_kernel(
-    depth, p_ref, g_ref, own_sem, zs, zr, xs, xr, ys, yr, ds, dr, cs, cr
-):
-    dp, z, x, core, y = place()
-    c_dev, x_dev, y_dev = partners(dp, x, core, y)
-    up_dev, down_dev = (dp + 4, y), (dp - 4, y)
-    own = pltpu.make_async_copy(p_ref, g_ref.at[:, z, x, core, y], own_sem)
-    own.start()
-    meet((c_dev, x_dev, y_dev), ((z + 1 < depth, up_dev), (z > 0, down_dev)))
-    own.wait()
-    steps = 2 * depth - 1
-
-    def target(q):
-        return z + ((q + 1) // 2) * (1 - 2 * (q % 2))
-
-    def z_copy(j, way, device):
-        slab = g_ref.at[:, j, x, core, y]
-        return send(slab, slab, zs.at[way, j], zr.at[j], device)
-
-    def x_copy(j):
-        slab = g_ref.at[:, j, x, core, y]
-        return send(slab, slab, xs.at[j], xr.at[j], x_dev)
-
-    def y_copy(j):
-        slab = g_ref.at[:, j, x, core, y]
-        return send(slab, slab, ys.at[j], yr.at[j], y_dev)
-
-    def d_copy(j, half):
-        if half == 0:
-            slab = g_ref.at[pl.ds(0, HALF), j, 1 - x, core, y]
-            return send(slab, slab, ds.at[0, j], dr.at[0, j], y_dev)
-        slab = g_ref.at[pl.ds(HALF, HALF), j, x, core, 1 - y]
-        return send(slab, slab, ds.at[1, j], dr.at[1, j], x_dev)
-
-    def c_copy(j, a, b):
-        slab = g_ref.at[:, j, (x + a) % 2, core, (y + b) % 2]
-        return send(slab, slab, cs.at[2 * a + b, j], cr.at[2 * a + b, j], c_dev)
-
-    def c_arrival(j, a, b):
-        slab = g_ref.at[:, j, (x + a) % 2, 1 - core, (y + b) % 2]
-        return send(slab, slab, cs.at[2 * a + b, j], cr.at[2 * a + b, j], c_dev)
-
-    def x_arrival(j):
-        slab = g_ref.at[:, j, 1 - x, core, y]
-        return send(slab, slab, xs.at[j], xr.at[j], x_dev)
-
-    def y_arrival(j):
-        slab = g_ref.at[:, j, x, core, 1 - y]
-        return send(slab, slab, ys.at[j], yr.at[j], y_dev)
-
-    def d_arrival(j, half):
-        slab = g_ref.at[pl.ds(half * HALF, HALF), j, 1 - x, core, 1 - y]
-        return send(slab, slab, ds.at[half, j], dr.at[half, j], y_dev if half == 0 else x_dev)
-
-    def first(j):
-        @pl.when(j != z)
-        def _():
-            z_copy(j, 0, up_dev).wait_recv()
-
-        @pl.when((j <= z) & (z + 1 < depth))
-        def _():
-            z_copy(j, 0, up_dev).start()
-
-        @pl.when((j >= z) & (z > 0))
-        def _():
-            z_copy(j, 1, down_dev).start()
-
-        x_copy(j).start()
-        y_copy(j).start()
-        c_copy(j, 0, 0).start()
-
-    def second(j):
-        x_arrival(j).wait_recv()
-        d_copy(j, 0).start()
-        c_copy(j, 1, 0).start()
-        y_arrival(j).wait_recv()
-        d_copy(j, 1).start()
-        c_copy(j, 0, 1).start()
-
-    def third(j):
-        d_arrival(j, 0).wait_recv()
-        d_arrival(j, 1).wait_recv()
-        c_copy(j, 1, 1).start()
-
-    def stage(q, work):
-        j = target(q)
-
-        @pl.when((q >= 0) & (q < steps) & (j >= 0) & (j < depth))
-        def _():
-            work(j)
-
-    def step(q, carry):
-        stage(q, first)
-        stage(q - 1, second)
-        stage(q - 2, third)
-        return carry
-
-    lax.fori_loop(0, steps + 2, step, 0)
-
-    def finish(j, carry):
-        for a in range(2):
-            for b in range(2):
-                c_arrival(j, a, b).wait_recv()
-                c_copy(j, a, b).wait_send()
-        x_copy(j).wait_send()
-        y_copy(j).wait_send()
-        d_copy(j, 0).wait_send()
-        d_copy(j, 1).wait_send()
-
-        @pl.when((j <= z) & (z + 1 < depth))
-        def _():
-            z_copy(j, 0, up_dev).wait_send()
-
-        @pl.when((j >= z) & (z > 0))
-        def _():
-            z_copy(j, 1, down_dev).wait_send()
-
-        return carry
-
-    lax.fori_loop(0, depth, finish, 0)
-
-
 def gather_all(packed, mesh):
-    dp, fsdp = mesh.shape["dp"], mesh.shape["fsdp"]
-    _, rows, width = packed.shape
-    if fsdp != 2 or dp % 4:
-        full = lax.all_gather(packed, ("dp", "fsdp"), axis=1, tiled=False)
-        return full.reshape(BLOCKS, dp * fsdp * rows, width)
-    depth = dp // 4
-    dma = pltpu.SemaphoreType.DMA
-    full = pl.pallas_call(
-        functools.partial(gather_kernel, depth),
-        out_shape=jax.ShapeDtypeStruct((BLOCKS, depth, 2, 2, 2, rows, width), packed.dtype),
-        in_specs=[pl.BlockSpec(memory_space=pltpu.VMEM)],
-        out_specs=pl.BlockSpec(memory_space=pl.ANY),
-        scratch_shapes=[
-            dma(()),
-            dma((2, depth)),
-            dma((depth,)),
-            dma((depth,)),
-            dma((depth,)),
-            dma((depth,)),
-            dma((depth,)),
-            dma((2, depth)),
-            dma((2, depth)),
-            dma((4, depth)),
-            dma((4, depth)),
-        ],
-        compiler_params=pltpu.CompilerParams(collective_id=0, has_side_effects=True),
-        name="gather_all",
-    )(packed)
-    return full.reshape(BLOCKS, dp * fsdp * rows, width)
+    if mesh is None:
+        return packed
+    full = lax.all_gather(packed, ("dp", "fsdp"), axis=1, tiled=False)
+    return full.reshape(BLOCKS, D, packed.shape[2])
 
 
 W = D // G
@@ -847,11 +700,17 @@
     return depth, kmt, gb
 
 
-def layer(mesh, hidden, lengths, full, out_grad):
+def layer(mesh, hidden, lengths, packed, out_grad):
     rows = hidden.shape[0]
     tokens = rows * SEQ
-    depth, kmt, gb = constants(full)
-    x, proj, dl, kc, wt, lse, ctx = forward(lengths, hidden, full, depth, kmt)
+    if fused(mesh, rows):
+        full, depth, kmt, gb, x, proj, dl, kc, wt, lse, ctx = gather_forward(
+            mesh, lengths, packed, hidden
+        )
+    else:
+        full = gather_all(packed, mesh)
+        depth, kmt, gb = constants(full)
+        x, proj, dl, kc, wt, lse, ctx = forward(lengths, hidden, full, depth, kmt)
     flat_x, flat_ctx = x.reshape(tokens, D), ctx.reshape(tokens, D)
     y, act, gpre, fb, gffn, gmix, gr1, gctx, stat = feed_forward(
         lengths, flat_ctx, flat_x, out_grad.reshape(tokens, D), full, gb
@@ -908,6 +767,415 @@
     pairs += [(x, gproj[b]) for b in range(4)]
     pairs += [(dl, gkc)]
     return jnp.stack([tn(a, b).astype(BF16) for a, b in pairs] + [small])
+
+
+def picked(height, rule):
+    row = lax.broadcasted_iota(jnp.int32, (height, 128), 0)
+    lane = lax.broadcasted_iota(jnp.int32, (height, 128), 1)
+    return rule(row, lane).astype(F32).astype(BF16)
+
+
+def gather_engine(depth, g_ref, low, high, sems):
+    dp, z, x, core, y = place()
+    c_dev, x_dev, y_dev = partners(dp, x, core, y)
+    up_dev, down_dev = (dp + 4, y), (dp - 4, y)
+    steps = 2 * depth - 1
+    size = (high - low) // 2
+    every, halves = pl.ds(low, 2 * size), (pl.ds(low, size), pl.ds(low + size, size))
+
+    def target(q):
+        return z + ((q + 1) // 2) * (1 - 2 * (q % 2))
+
+    def z_copy(j, way, device):
+        slab = g_ref.at[every, j, x, core, y]
+        return send(slab, slab, sems[0].at[way, j], sems[1].at[j], device)
+
+    def x_copy(j):
+        slab = g_ref.at[every, j, x, core, y]
+        return send(slab, slab, sems[2].at[j], sems[3].at[j], x_dev)
+
+    def y_copy(j):
+        slab = g_ref.at[every, j, x, core, y]
+        return send(slab, slab, sems[4].at[j], sems[5].at[j], y_dev)
+
+    def d_copy(j, half):
+        if half == 0:
+            slab = g_ref.at[halves[0], j, 1 - x, core, y]
+            return send(slab, slab, sems[6].at[0, j], sems[7].at[0, j], y_dev)
+        slab = g_ref.at[halves[1], j, x, core, 1 - y]
+        return send(slab, slab, sems[6].at[1, j], sems[7].at[1, j], x_dev)
+
+    def c_copy(j, a, b):
+        slab = g_ref.at[every, j, (x + a) % 2, core, (y + b) % 2]
+        return send(slab, slab, sems[8].at[2 * a + b, j], sems[9].at[2 * a + b, j], c_dev)
+
+    def c_arrival(j, a, b):
+        slab = g_ref.at[every, j, (x + a) % 2, 1 - core, (y + b) % 2]
+        return send(slab, slab, sems[8].at[2 * a + b, j], sems[9].at[2 * a + b, j], c_dev)
+
+    def x_arrival(j):
+        slab = g_ref.at[every, j, 1 - x, core, y]
+        return send(slab, slab, sems[2].at[j], sems[3].at[j], x_dev)
+
+    def y_arrival(j):
+        slab = g_ref.at[every, j, x, core, 1 - y]
+        return send(slab, slab, sems[4].at[j], sems[5].at[j], y_dev)
+
+    def d_arrival(j, half):
+        slab = g_ref.at[halves[half], j, 1 - x, core, 1 - y]
+        return send(slab, slab, sems[6].at[half, j], sems[7].at[half, j], y_dev if half == 0 else x_dev)
+
+    def first(j):
+        @pl.when(j != z)
+        def _():
+            z_copy(j, 0, up_dev).wait_recv()
+
+        @pl.when((j <= z) & (z + 1 < depth))
+        def _():
+            z_copy(j, 0, up_dev).start()
+
+        @pl.when((j >= z) & (z > 0))
+        def _():
+            z_copy(j, 1, down_dev).start()
+
+        x_copy(j).start()
+        y_copy(j).start()
+        c_copy(j, 0, 0).start()
+
+    def second(j):
+        x_arrival(j).wait_recv()
+        d_copy(j, 0).start()
+        c_copy(j, 1, 0).start()
+        y_arrival(j).wait_recv()
+        d_copy(j, 1).start()
+        c_copy(j, 0, 1).start()
+
+    def third(j):
+        d_arrival(j, 0).wait_recv()
+        d_arrival(j, 1).wait_recv()
+        c_copy(j, 1, 1).start()
+
+    def stage(q, work):
+        j = target(q)
+
+        @pl.when((q >= 0) & (q < steps) & (j >= 0) & (j < depth))
+        def _():
+            work(j)
+
+    def arrive(j, carry):
+        for a in range(2):
+            for b in range(2):
+                c_arrival(j, a, b).wait_recv()
+        return carry
+
+    def step(q, carry):
+        stage(q, first)
+        stage(q - 1, second)
+        stage(q - 2, third)
+        return carry
+
+    def finish(j, carry):
+        for a in range(2):
+            for b in range(2):
+                c_copy(j, a, b).wait_send()
+        x_copy(j).wait_send()
+        y_copy(j).wait_send()
+        d_copy(j, 0).wait_send()
+        d_copy(j, 1).wait_send()
+
+        @pl.when((j <= z) & (z + 1 < depth))
+        def _():
+            z_copy(j, 0, up_dev).wait_send()
+
+        @pl.when((j >= z) & (z > 0))
+        def _():
+            z_copy(j, 1, down_dev).wait_send()
+
+        return carry
+
+    return step, arrive, finish
+
+
+def gather_forward_kernel(
+    depth,
+    len_ref,
+    p_ref,
+    hid_hbm,
+    g_ref,
+    taps_ref,
+    kmt_ref,
+    gb_ref,
+    x_out,
+    proj_out,
+    dl_out,
+    kc_out,
+    wt_out,
+    lse_out,
+    ctx_out,
+    hid_ref,
+    x_ref,
+    proj_ref,
+    dl_ref,
+    kc_ref,
+    wt_ref,
+    lse_ref,
+    ctx_ref,
+    win_ref,
+    wpt_ref,
+    small_ref,
+    small,
+    xs,
+    sv,
+    ot,
+    own_sem,
+    in_sem,
+    out_sem,
+    *sems,
+):
+    dp, z, x, core, y = place()
+    rows = hid_ref.shape[0]
+    depth_ref = taps_ref
+    load = pltpu.make_async_copy(hid_hbm, hid_ref, in_sem.at[0])
+    load.start()
+    own = pltpu.make_async_copy(p_ref, g_ref.at[:, z, x, core, y], own_sem)
+    own.start()
+    xs[0:PAD] = jnp.zeros((PAD, D), F32)
+    xs[PAD + SEQ :] = jnp.zeros((PAD, D), F32)
+    sv[0:PAD] = jnp.zeros((PAD, W), F32)
+    sv[PAD + SEQ :] = jnp.zeros((PAD, W), F32)
+    meet(
+        partners(dp, x, core, y),
+        ((z + 1 < depth, (dp + 4, y)), (z > 0, (dp - 4, y))),
+    )
+    own.wait()
+    count = len(sems) // 2
+    soon = gather_engine(depth, g_ref, 10, 16, sems[:count])
+    later = gather_engine(depth, g_ref, 0, 10, sems[count:])
+    lax.fori_loop(0, 2 * depth + 1, soon[0], 0)
+    lax.fori_loop(0, depth, soon[1], 0)
+    inputs = [
+        pltpu.make_async_copy(g_ref.at[pl.ds(first, size)], target, in_sem.at[1 + i])
+        for i, (first, size, target) in enumerate(
+            ((15, 1, small_ref), (10, 4, win_ref), (14, 1, wpt_ref))
+        )
+    ]
+    for copy in inputs:
+        copy.start()
+    later[0](0, 0)
+    load.wait()
+    inputs[0].wait()
+    values = small_ref[...].reshape(D, W)[:, 0:128]
+    small[...] = values.astype(F32)
+    taps_ref[...] = nt(picked(16, lambda row, lane: (row < K) & (lane == row)), values)
+    gb_ref[...] = nt(picked(8, lambda row, lane: (row < 4) & (lane == row + 4 * K)), values)
+    kernel = jnp.zeros((8 * K, W), F32)
+    for odd in range(2):
+        pick = picked(
+            8 * K,
+            lambda row, lane: (row % 8 >= 3 * odd)
+            & (row % 8 < 3 * odd + 3)
+            & (lane == K + row // 8 * 3 + row % 8 - 3 * odd),
+        )
+        kernel = kernel + nt(pick, small[pl.ds(odd, W, stride=2)].astype(BF16))
+    kmt_ref[...] = kernel.astype(BF16)
+    for copy in inputs[1:]:
+        copy.wait()
+
+    def inside_of(r):
+        return lax.broadcasted_iota(jnp.int32, (SEQ, 1), 0) < len_ref[r]
+
+    def piece_project(r):
+        inside = inside_of(r)
+        x = jnp.where(inside, hid_ref[r], jnp.zeros((), BF16))
+        x_ref[r] = x
+        xs[PAD : PAD + SEQ] = x.astype(F32)
+
+        for b in range(4):
+            part = nn(x_ref[r], win_ref[b].reshape(D, W)).astype(BF16)
+            proj_ref[r, :, b * W : (b + 1) * W] = part
+            if b == 3:
+                sv[PAD : PAD + SEQ] = part.astype(F32)
+
+    def piece_columns(r):
+        def column(c, carry):
+            lane = pl.ds(pl.multiple_of(c * 128, 128), 128)
+            for n in range(8):
+                total = jnp.zeros((64, 128), F32)
+                for k in range(K):
+                    start = PAD + n * 64 + k - K // 2
+                    total = total + xs[start : start + 64, lane] * depth_ref[k : k + 1, lane]
+                dl_ref[r, n * 64 : (n + 1) * 64, lane] = total.astype(BF16)
+            return carry
+
+        lax.fori_loop(0, D // 128, column, 0)
+
+    def piece_span(r):
+        kc_ref[r] = nn(dl_ref[r], wpt_ref[0].reshape(D, W))
+        mk = (kc_ref[r] * proj_ref[r, :, 0:W].astype(F32)).astype(BF16)
+        logits = nt(kmt_ref[...], mk)
+        top = logits[0:8]
+        for k in range(1, K):
+            top = jnp.maximum(top, logits[k * 8 : k * 8 + 8])
+        parts = [jnp.exp(logits[k * 8 : k * 8 + 8] - top) for k in range(K)]
+        inverse = 1.0 / sum(parts)
+        both = []
+        for k in range(K):
+            weight = parts[k] * inverse
+            wt_ref[r, k * 8 : k * 8 + 8] = weight
+            high = weight.astype(BF16).astype(F32)
+            both.append(jnp.concatenate([high, weight - high], axis=0).astype(BF16))
+        e16 = spread(16)
+        for n in range(4):
+            total = jnp.zeros((128, W), F32)
+            for k in range(K):
+                start = PAD + n * 128 + k - K // 2
+                total = total + tn(both[k][:, n * 128 : (n + 1) * 128], e16) * sv[start : start + 128]
+            ctx_ref[r, n * 128 : (n + 1) * 128, W:] = total.astype(BF16)
+
+    def piece_pairs(r, first, stop):
+        inside = inside_of(r)
+        lane_head = lax.broadcasted_iota(jnp.int32, (1, 128), 1) // HD
+        bias = jnp.where(inside, 0.0, -1e30).astype(F32)
+
+        def pair(p, carry):
+            def slab(part):
+                return proj_ref[r, :, pl.ds(pl.multiple_of(part * W + p * 128, 128), 128)]
+
+            q2, k2, v2 = slab(0), slab(1), slab(2)
+            for h in range(2):
+                scale = jnp.where(lane_head == h, 1.0 / math.sqrt(HD), 0.0).astype(BF16)
+                scores = nt(k2, q2 * scale) + bias
+                peak = jnp.max(scores, axis=0, keepdims=True)
+                power = jnp.exp(scores - peak)
+                total = jnp.sum(power, axis=0, keepdims=True)
+                lse_ref[r, pl.ds(p * 2 + h, 1)] = peak + jnp.log(total)
+                probs = (power * (1.0 / total)).astype(BF16)
+                ot[h * HD : (h + 1) * HD] = tn(v2, probs)[h * HD : (h + 1) * HD]
+            ctx_ref[r, :, pl.ds(pl.multiple_of(p * 128, 128), 128)] = ot[...].T.astype(BF16)
+            return carry
+
+        lax.fori_loop(first, stop, pair, 0)
+
+
+    pairs = (
+        (x_ref, x_out),
+        (proj_ref, proj_out),
+        (dl_ref, dl_out),
+        (kc_ref, kc_out),
+        (wt_ref, wt_out),
+        (lse_ref, lse_out),
+        (ctx_ref, ctx_out),
+    )
+
+    def store(r):
+        return [
+            pltpu.make_async_copy(source.at[r], target.at[r], out_sem.at[i, r])
+            for i, (source, target) in enumerate(pairs)
+        ]
+
+    def tick(t, carry):
+        row = t // 5
+
+        def when(i, work):
+            @pl.when(t % 5 == i)
+            def _():
+                work()
+
+        when(0, lambda: piece_project(row))
+        when(1, lambda: piece_columns(row))
+        when(2, lambda: piece_span(row))
+        when(3, lambda: piece_pairs(row, 0, 2))
+
+        def close():
+            piece_pairs(row, 2, 3)
+            for copy in store(row):
+                copy.start()
+
+        when(4, close)
+
+        @pl.when(t < 2 * depth)
+        def _():
+            later[0](t + 1, 0)
+
+        return carry
+
+    lax.fori_loop(0, 5 * rows, tick, 0)
+    for t in range(5 * rows, 2 * depth):
+        later[0](jnp.int32(t + 1), 0)
+    lax.fori_loop(0, depth, later[1], 0)
+    lax.fori_loop(0, depth, soon[2], 0)
+    lax.fori_loop(0, depth, later[2], 0)
+
+    def drain(r, carry):
+        for copy in store(r):
+            copy.wait()
+        return carry
+
+    lax.fori_loop(0, rows, drain, 0)
+
+
+def gather_forward(mesh, lengths, packed, hidden):
+    dp, fsdp = mesh.shape["dp"], mesh.shape["fsdp"]
+    _, share, _ = packed.shape
+    depth = dp // 4
+    rows = hidden.shape[0]
+    dma = pltpu.SemaphoreType.DMA
+    anywhere = pl.BlockSpec(memory_space=pl.ANY)
+    inside = pl.BlockSpec(memory_space=pltpu.VMEM)
+    kinds = (
+        (BF16, SEQ, D),
+        (BF16, SEQ, 4 * W),
+        (BF16, SEQ, D),
+        (F32, SEQ, W),
+        (F32, 8 * K, SEQ),
+        (F32, 8, SEQ),
+        (BF16, SEQ, D),
+    )
+    sems = [
+        dma((2, depth)),
+        dma((depth,)),
+        dma((depth,)),
+        dma((depth,)),
+        dma((depth,)),
+        dma((depth,)),
+        dma((2, depth)),
+        dma((2, depth)),
+        dma((4, depth)),
+        dma((4, depth)),
+    ]
+    outs = pl.pallas_call(
+        functools.partial(gather_forward_kernel, depth),
+        out_shape=(
+            jax.ShapeDtypeStruct((BLOCKS, depth, 2, 2, 2, share, W), BF16),
+            jax.ShapeDtypeStruct((16, D), F32),
+            jax.ShapeDtypeStruct((8 * K, W), BF16),
+            jax.ShapeDtypeStruct((8, D), F32),
+        )
+        + tuple(jax.ShapeDtypeStruct((rows, a, b), kind) for kind, a, b in kinds),
+        in_specs=[pl.BlockSpec(memory_space=pltpu.SMEM), inside, anywhere],
+        out_specs=(anywhere, inside, inside, inside) + (anywhere,) * 7,
+        scratch_shapes=[pltpu.VMEM((rows, SEQ, D), BF16)]
+        + [pltpu.VMEM((rows, a, b), kind) for kind, a, b in kinds]
+        + [
+            pltpu.VMEM((4, depth, 2, 2, 2, share, W), BF16),
+            pltpu.VMEM((1, depth, 2, 2, 2, share, W), BF16),
+            pltpu.VMEM((1, depth, 2, 2, 2, share, W), BF16),
+            pltpu.VMEM((D, 128), F32),
+            pltpu.VMEM((SEQ + 2 * PAD, D), F32),
+            pltpu.VMEM((SEQ + 2 * PAD, W), F32),
+            pltpu.VMEM((128, SEQ), F32),
+            dma(()),
+            dma((4,)),
+            dma((7, rows)),
+        ]
+        + sems
+        + sems,
+        compiler_params=pltpu.CompilerParams(
+            collective_id=0, has_side_effects=True, vmem_limit_bytes=56 * 1024 * 1024
+        ),
+        name="gather_forward",
+    )(lengths, packed, hidden)
+    return (outs[0].reshape(BLOCKS, D, W),) + tuple(outs[1:])
 
 
 def backward_scatter_kernel(
@@ -1543,8 +1811,7 @@
     norm_biases,
     out_grad,
 ):
-    full = gather_all(
-        pack(
+    packed = pack(
             in_weight,
             depth_kernel,
             point_weight,
@@ -1554,10 +1821,8 @@
             down_weight,
             norm_gains,
             norm_biases,
-        ),
-        mesh,
     )
-    output, input_grad, shard, totals = layer(mesh, hidden, lengths, full, out_grad)
+    output, input_grad, shard, totals = layer(mesh, hidden, lengths, packed, out_grad)
     rms = jnp.sqrt(totals[0, :4] / (totals[0, 4] * D))
     return (output, input_grad) + unpack(shard) + (rms,)
 

time: 275 us -> 267 us (0.971)
  local copies, waits for them, and re-layouts: 24.4 us -> 19.2 us
    pallas_call x2 -> x1, Pallas kernels: 78.9 us -> 76.9 us  [gather_forward(): pl.pallas_call(functools.partial(gather_forward_kernel, depth), out_shape...]
    unnamed x20 -> x19, local copies, waits for them, and re-layouts: 13.2 us -> 12.6 us
where the time goes in v4:
time: 267 us
  Pallas kernels  245 us (92%)
  local copies, waits for them, and re-layouts  19.2 us (7%)
    pallas_call x1, Pallas kernels, backward_scatter(): pl.pallas_call(functools.partial(backward_scatter_kernel, depth), out_sha...  103 us
    pallas_call x1, Pallas kernels, gather_forward(): pl.pallas_call(functools.partial(gather_forward_kernel, depth), out_shape...  76.9 us
    pallas_call x1, Pallas kernels, feed_forward(): pl.pallas_call(ffn_kernel, grid=(tokens // TILE,), out_shape=(out(BF16, D...  64.3 us
    unnamed x19, local copies, waits for them, and re-layouts  12.6 us

profile of v4, /device:TPU:0, one launch (start us, length us, event | category | flops | bytes accessed | tf_op | source)
XLA Modules:
  0.0 266.5 jit_solution(6139908543690656588)
XLA Ops:
  0.6 0.8 copy.34
  1.4 0.7 copy.37
  2.2 0.7 copy.38
  2.9 0.8 copy.35
  3.7 0.1 copy.36
  3.9 0.1 copy.39
  4.0 0.9 constant_dynamic-update-slice_fusion.1
  4.9 0.9 constant_dynamic-update-slice_fusion
  5.8 0.8 fusion.1
  6.5 0.9 fusion
  7.4 0.7 bitcast_dynamic-update-slice_fusion
  8.2 0.1 fusion.10.p_ref
  8.3 0.7 copy-done.1
  9.0 76.9 %gather_forward.1 = (bf16[16,4,2,2,2,24,384]{6,5,4,3,2,1,0:T(8,128)(2,1)}, f32[16,768]{1,0:T(8,128)}, bf16[72,384]{1,0:T(8,128)(2,1)}, f32[8,768]{1,0:T(8,128)},...) custom-call(s32[2]{0:T(128)} %len_ref.5, ...), custom_call_target="tpu_custom_call" | custom-call | tf_op jit(solution)/shard_map/gather_forward/pallas_call | solution.py:1146
  85.9 64.3 %feed_forward.1 = (bf16[1024,768]{1,0:T(8,128)(2,1)}, bf16[4,1024,768]{2,1,0:T(8,128)(2,1)}, bf16[4,1024,768]{2,1,0:T(8,128)(2,1)}, bf16[2,1024,384]{2,1,0:T(8,1...) custom-call(s32[2]{0:T(128)} %len_ref.5, ...), custom_call_target="tpu_custom_call" | custom-call | tf_op jit(solution)/shard_map/feed_forward/pallas_call | solution.py:408
  150.2 103.5 %backward_scatter.1 = (bf16[2,512,768]{2,1,0:T(8,128)(2,1)}, f32[16,24,384]{2,1,0:T(8,128)}, f32[8,128]{1,0:T(8,128)}) custom-call(s32[2]{0:T(128)} %len_ref.5, bf16[2,512,768]{2,1,0:T(8,128)(2,1)} %get-tuple-element.36.x_hbm, bf16[2,512,1536]{2,1,0:T(8,128)(2,1)} %get-tuple-element.40.proj_hbm, bf16[2,512,768]{2,1,0:T(8,128)(2,1)} %get-tuple-element.41.dl_hbm, ...), custom_call_target="tpu_custom_call" | custom-call | tf_op jit(solution)/shard_map/backward_scatter/pallas_call | solution.py:1719
  253.7 1.4 slice.47
  255.7 1.2 sqrt_bitcast_fusion
  256.9 0.9 slice_bitcast_fusion.1
  257.8 0.6 copy.51
  258.5 1.4 slice_bitcast_fusion.2
  259.9 1.8 fusion.11
  261.7 0.1 slice.49
  261.7 0.1 copy.41
  261.9 0.1 slice_bitcast_fusion.4
  261.9 0.7 copy.44
  262.6 0.6 copy.47
  263.2 0.6 copy.46
  263.9 0.1 copy.42
  264.0 0.7 copy.45
  264.7 0.7 copy.50
  265.4 1.1 copy.60
  (8 shorter events, 0.1 us)
Async XLA Ops:
  8.3 0.7 copy-start.1
  253.7 11.7 %copy-start = (bf16[2,512,768]{2,1,0:T(8,128)(2,1)S(1)}, bf16[2,512,768]{2,1,0:T(8,128)(2,1)}, u32[]{:S(2)}) copy-start(bf16[2,512,768]{2,1,0:T(8,128)(2,1)} %get-tuple-element.102) | copy-start | bytes 4718596

commit v5 on v4

--- a/solution.py
+++ b/solution.py
@@ -228,7 +228,7 @@
 
 
 TILE = 256
-CHUNK = 16
+CHUNK = 256
 PART = 256
 
 
@@ -951,7 +951,9 @@
     count = len(sems) // 2
     soon = gather_engine(depth, g_ref, 10, 16, sems[:count])
     later = gather_engine(depth, g_ref, 0, 10, sems[count:])
-    lax.fori_loop(0, 2 * depth + 1, soon[0], 0)
+    lax.fori_loop(0, 2 * depth - 1, soon[0], 0)
+    later[0](0, 0)
+    lax.fori_loop(2 * depth - 1, 2 * depth + 1, soon[0], 0)
     lax.fori_loop(0, depth, soon[1], 0)
     inputs = [
         pltpu.make_async_copy(g_ref.at[pl.ds(first, size)], target, in_sem.at[1 + i])
@@ -961,7 +963,6 @@
     ]
     for copy in inputs:
         copy.start()
-    later[0](0, 0)
     load.wait()
     inputs[0].wait()
     values = small_ref[...].reshape(D, W)[:, 0:128]

time: 267 us -> 227 us (0.85)
  Pallas kernels: 245 us -> 204 us
    pallas_call x1, Pallas kernels: 64.3 us -> 30.6 us  [feed_forward(): pl.pallas_call(ffn_kernel, grid=(tokens // TILE,), out_shape=(out(BF16, D...]
    pallas_call x1, Pallas kernels: 76.9 us -> 72.1 us  [gather_forward(): pl.pallas_call(functools.partial(gather_forward_kernel, depth), out_shape...]
where the time goes in v5:
time: 227 us; the launch traced here: 226 us
  Pallas kernels  204 us (90%)
  local copies, waits for them, and re-layouts  19.2 us (8%)
    pallas_call x1, Pallas kernels, backward_scatter(): pl.pallas_call(functools.partial(backward_scatter_kernel, depth), out_sha...  102 us
    pallas_call x1, Pallas kernels, gather_forward(): pl.pallas_call(functools.partial(gather_forward_kernel, depth), out_shape...  72.1 us
    pallas_call x1, Pallas kernels, feed_forward(): pl.pallas_call(ffn_kernel, grid=(tokens // TILE,), out_shape=(out(BF16, D...  30.6 us
    unnamed x19, local copies, waits for them, and re-layouts  12.6 us

profile of v5, /device:TPU:0, one launch (start us, length us, event | category | flops | bytes accessed | tf_op | source)
XLA Modules:
  0.0 226.1 jit_solution(10729533304472008004)
XLA Ops:
  0.6 0.8 copy.34
  1.4 0.7 copy.37
  2.2 0.7 copy.38
  2.9 0.8 copy.35
  3.7 0.1 copy.36
  3.9 0.1 copy.39
  4.0 0.9 constant_dynamic-update-slice_fusion.1
  4.9 0.9 constant_dynamic-update-slice_fusion
  5.8 0.8 fusion.1
  6.5 0.9 fusion
  7.4 0.7 bitcast_dynamic-update-slice_fusion
  8.2 0.1 fusion.10.p_ref
  8.3 0.7 copy-done.1
  9.0 72.1 %gather_forward.1 = (bf16[16,4,2,2,2,24,384]{6,5,4,3,2,1,0:T(8,128)(2,1)}, f32[16,768]{1,0:T(8,128)}, bf16[72,384]{1,0:T(8,128)(2,1)}, f32[8,768]{1,0:T(8,128)},...) custom-call(s32[2]{0:T(128)} %len_ref.5, ...), custom_call_target="tpu_custom_call" | custom-call | tf_op jit(solution)/shard_map/gather_forward/pallas_call | solution.py:1147
  81.0 30.6 %feed_forward.1 = (bf16[1024,768]{1,0:T(8,128)(2,1)}, bf16[4,1024,768]{2,1,0:T(8,128)(2,1)}, bf16[4,1024,768]{2,1,0:T(8,128)(2,1)}, bf16[2,1024,384]{2,1,0:T(8,1...) custom-call(s32[2]{0:T(128)} %len_ref.5, ...), custom_call_target="tpu_custom_call" | custom-call | tf_op jit(solution)/shard_map/feed_forward/pallas_call | solution.py:408
  111.6 101.7 %backward_scatter.1 = (bf16[2,512,768]{2,1,0:T(8,128)(2,1)}, f32[16,24,384]{2,1,0:T(8,128)}, f32[8,128]{1,0:T(8,128)}) custom-call(s32[2]{0:T(128)} %len_ref.5, bf16[2,512,768]{2,1,0:T(8,128)(2,1)} %get-tuple-element.36.x_hbm, bf16[2,512,1536]{2,1,0:T(8,128)(2,1)} %get-tuple-element.40.proj_hbm, bf16[2,512,768]{2,1,0:T(8,128)(2,1)} %get-tuple-element.41.dl_hbm, ...), custom_call_target="tpu_custom_call" | custom-call | tf_op jit(solution)/shard_map/backward_scatter/pallas_call | solution.py:1720
  213.3 1.4 slice.47
  215.4 1.2 sqrt_bitcast_fusion
  216.6 0.9 slice_bitcast_fusion.1
  217.5 0.6 copy.51
  218.1 1.4 slice_bitcast_fusion.2
  219.5 1.8 fusion.11
  221.3 0.1 slice.49
  221.4 0.1 copy.41
  221.5 0.1 slice_bitcast_fusion.4
  221.6 0.7 copy.44
  222.2 0.6 copy.47
  222.9 0.6 copy.46
  223.5 0.1 copy.42
  223.6 0.7 copy.45
  224.3 0.7 copy.50
  225.0 1.1 copy.60
  (8 shorter events, 0.1 us)
Async XLA Ops:
  8.3 0.7 copy-start.1
  213.3 11.7 %copy-start = (bf16[2,512,768]{2,1,0:T(8,128)(2,1)S(1)}, bf16[2,512,768]{2,1,0:T(8,128)(2,1)}, u32[]{:S(2)}) copy-start(bf16[2,512,768]{2,1,0:T(8,128)(2,1)} %get-tuple-element.102) | copy-start | bytes 4718596
